TPU v7x, 32 devices: a whole 2x2x4 slice. The times are simulated.
32 devices in a mesh: north: 4 (over y, x), east: 8 (over z, core).
Axes of the slice: x: 2, y: 2, z: 4, core: 2. Of those that a mesh axis runs over, the one named last changes fastest.
Arguments:
- pair_rows: bfloat16 [96, 96, 128], P('north', 'east'), may hold values from -6 to 6
- in_gain: float32 [128], replicated, may hold values from 0.25 to 1.75
- left_weight: bfloat16 [128, 128], replicated, may hold values from -0.5 to 0.5
- right_weight: bfloat16 [128, 128], replicated, may hold values from -0.5 to 0.5
- left_gate: bfloat16 [128, 128], replicated, may hold values from -0.5 to 0.5
- right_gate: bfloat16 [128, 128], replicated, may hold values from -0.5 to 0.5
- mid_gain: float32 [128], replicated, may hold values from 0.25 to 1.75
- out_weight: bfloat16 [128, 128], replicated, may hold values from -0.5 to 0.5
- out_gate: bfloat16 [128, 128], replicated, may hold values from -0.5 to 0.5
Outputs:
- pair_change: bfloat16 [96, 96, 128], P('north', 'east')
All inputs are finite; a program needn't handle non-finite values.
Results may differ from a plain program's by a relative error of at most 0.012.
Values may be sent and summed in bfloat16 or wider, within the bound.
No kernel may reach another device: no remote copies, remote signals or barrier semaphores. Data moves between devices by JAX's collectives and lax.ppermute only.
A program may use at most 128 MiB of HBM per device.

v0:
```python
import math

import jax
import jax.numpy as jnp
from jax import lax
from jax.experimental import pallas as pl
from jax.experimental.pallas import tpu as pltpu
from jax.sharding import PartitionSpec as P


F32, BF16 = jnp.float32, jnp.bfloat16
CORES = 2
VMEM = pl.BlockSpec(memory_space=pltpu.VMEM)
HBM = pl.BlockSpec(memory_space=pltpu.HBM)


def scale_channels(values, channel_gain):
    centred = values - jnp.mean(values, axis=-1, keepdims=True)
    return (
        centred
        * lax.rsqrt(jnp.mean(centred * centred, axis=-1, keepdims=True) + 1e-05)
        * channel_gain
    )


def dot(a, b):
    return jnp.dot(a, b, preferred_element_type=F32)


def shape(dims, dtype=BF16):
    return jax.ShapeDtypeStruct(tuple(dims), dtype)


def call(kernel, outs, specs, args, us, scratch=()):
    tree = jax.tree.map(lambda _: VMEM, outs)
    live = sum(math.prod(a.shape) * a.dtype.itemsize for a in (*jax.tree.leaves(outs), *args))
    live += sum(math.prod(s.shape) * 4 for s in scratch if s.memory_space == pltpu.VMEM)
    return pl.pallas_call(
        kernel,
        out_shape=outs,
        in_specs=specs,
        out_specs=tree,
        scratch_shapes=list(scratch),
        cost_estimate=pl.CostEstimate(flops=int(us * 16e6), bytes_accessed=0, transcendentals=0),
        compiler_params=pltpu.CompilerParams(vmem_limit_bytes=min((8 << 20) + 2 * live, 60 << 20)),
    )(*args)


def ready_of(x_ref, gain):
    width, height, channels = x_ref.shape
    x = x_ref[...].astype(F32).reshape(width * height, channels)
    return scale_channels(x, gain).astype(BF16)


def gated(ready, weight_ref, gate_ref):
    return (dot(ready, weight_ref[...]) * jax.nn.sigmoid(dot(ready, gate_ref[...]))).astype(BF16)


def own_kernel(n_copies, pitch, *refs):
    x_hbm, og_hbm = refs[:2]
    sources = refs[2 : 2 + n_copies]
    ready_ref, gate_ref, right_ref, turn_ref = refs[2 + n_copies : 6 + n_copies]
    copies = refs[6 + n_copies : 6 + 2 * n_copies]
    x_ref, og_ref, sems = refs[6 + 2 * n_copies :]
    moves = [
        pltpu.make_async_copy(source, target, sems.at[i])
        for i, (source, target) in enumerate(
            zip((x_hbm, og_hbm, *sources), (x_ref, og_ref, *copies), strict=True)
        )
    ]
    for move in moves:
        move.start()
    width, height, _ = x_ref.shape
    columns = turn_ref.shape[2]
    core = lax.rem(lax.axis_index("east"), CORES)
    row = lax.broadcasted_iota(jnp.int32, (height, columns), 0)
    column = lax.broadcasted_iota(jnp.int32, (height, columns), 1)
    for half in range(CORES):
        offset = half * (pitch - width)
        at = core if half == 0 else 1 - core
        for j in range(width):
            hit = jnp.zeros((height, columns), F32)
            for r in range(height // (CORES * width)):
                first = (r * CORES + at) * width
                inside = (row >= first) & (row < first + width)
                same = column == (row - first + r * width) * pitch + (j + offset)
                hit = jnp.where(inside & same, 1.0, hit)
            turn_ref[half, pl.ds(j * height, height), :] = hit.astype(BF16)
    for move in moves:
        move.wait()
    gain_ref, _, _, _, rw_ref, rg_ref, _ = copies
    ready = ready_of(x_ref, gain_ref[...])
    ready_ref[...] = ready
    gate_ref[...] = jax.nn.sigmoid(dot(ready, og_ref[...]))
    right_ref[...] = gated(ready, rw_ref, rg_ref).astype(F32)


def mix(out_ref, left_ref, right_ref):
    height, tiles_j, _, channels = right_ref.shape
    width = out_ref.shape[0]
    tile_j = 3 if tiles_j % 3 == 0 else 1
    tile_i = 12 if width % 12 == 0 else 4
    step = 8
    for i0 in range(0, width, tile_i):
        for j0 in range(0, tiles_j, tile_j):

            def some(kk, total, i0=i0, j0=j0):
                total = list(total)
                for dk in range(step):
                    k = kk * step + dk
                    right = right_ref[k, pl.ds(j0, tile_j)]
                    for i in range(tile_i):
                        start = (i0 + i) * height + k
                        total[i] = total[i] + right * left_ref[pl.ds(start, 8, stride=0), :][None]
                return tuple(total)

            zero = jnp.zeros((tile_j, 8, channels), F32)
            total = lax.fori_loop(0, height // step, some, (zero,) * tile_i, unroll=height <= 24)
            for i in range(tile_i):
                out_ref[i0 + i, pl.ds(j0 * 8, tile_j * 8), :] = (
                    total[i].reshape(tile_j * 8, channels).astype(BF16)
                )


def first_kernel(
    x_ref, gain_ref, lw_ref, lg_ref, rw_ref, rg_ref, ready_ref, own_ref, right_ref, part_ref, flat_ref, left_ref
):
    pairs = own_ref.shape[0]
    height, tiles_j, _, channels = right_ref.shape
    flat_ref[pl.ds(0, pairs), :] = own_ref[...]
    other = gated(ready_of(x_ref, gain_ref[...]), rw_ref, rg_ref)
    flat_ref[pl.ds(pairs, pairs), :] = other.astype(F32)
    for k in range(height):
        right_ref[k] = flat_ref[pl.ds(k, tiles_j * 8, stride=height), :].reshape(tiles_j, 8, channels)
    left_ref[...] = gated(ready_ref[...], lw_ref, lg_ref).astype(F32)
    mix(part_ref, left_ref, right_ref)


def next_kernel(x_ref, gain_ref, lw_ref, lg_ref, right_ref, part_ref, left_ref):
    left_ref[...] = gated(ready_of(x_ref, gain_ref[...]), lw_ref, lg_ref).astype(F32)
    mix(part_ref, left_ref, right_ref)


def last_kernel(levels, rows, *refs):
    x_ref, gain_ref, lw_ref, lg_ref, right_ref = refs[:5]
    parts = refs[5 : 4 + levels]
    outs = refs[4 + levels : 4 + levels + rows]
    all_ref, left_ref = refs[4 + levels + rows :]
    level, row = lax.div(lax.axis_index("east"), CORES), lax.axis_index("north")
    left_ref[...] = gated(ready_of(x_ref, gain_ref[...]), lw_ref, lg_ref).astype(F32)
    mix(all_ref.at[levels - 1], left_ref, right_ref)
    for s, ref in enumerate(parts):
        all_ref[s] = ref[...]
    per_row = levels // rows
    width = all_ref.shape[1]
    for a, out_ref in enumerate(outs):
        for r in range(per_row):
            s = lax.rem(level - ((row ^ a) * per_row + r) + levels, levels)
            out_ref[pl.ds(r * width, width)] = all_ref[s]


def sum_kernel(scale, gain_ref, *refs):
    parts, (keep_ref, send_ref) = refs[:-2], refs[-2:]
    total = parts[0][...].astype(F32)
    for ref in parts[1:]:
        total = total + ref[...].astype(F32)
    mixed = (total * scale).astype(BF16).astype(F32)
    channels = mixed.shape[2]
    scaled = scale_channels(mixed, gain_ref[...].reshape(1, 1, channels)).astype(BF16)
    pitch = keep_ref.shape[1]
    keep_ref[...] = scaled[:, :pitch]
    send_ref[...] = scaled[:, scaled.shape[1] - pitch :]


def turned(half_ref, turn_ref, which, weight_ref):
    rows, pitch, channels = half_ref.shape
    half = half_ref[...].reshape(rows * pitch, channels)
    return dot(dot(turn_ref[which], half).astype(BF16), weight_ref[...])


def keep_kernel(keep_ref, turn_ref, weight_ref, out_ref):
    out_ref[...] = turned(keep_ref, turn_ref, 0, weight_ref)


def out_kernel(come_ref, turn_ref, weight_ref, kept_ref, gate_ref, out_ref):
    out = (kept_ref[...] + turned(come_ref, turn_ref, 1, weight_ref)) * gate_ref[...]
    out_ref[...] = out.astype(BF16).reshape(out_ref.shape)


def body(
    pair_rows,
    in_gain,
    left_weight,
    right_weight,
    left_gate,
    right_gate,
    mid_gain,
    out_weight,
    out_gate,
):
    rows, blocks = lax.axis_size("north"), lax.axis_size("east")
    levels = blocks // CORES
    per_row = levels // rows
    height, width, channels = pair_rows.shape
    mix_width = left_weight.shape[1]
    both, pairs, part_rows = CORES * width, width * height, per_row * width
    pitch = both - width // 8 * 8
    assert levels == per_row * rows and rows & (rows - 1) == 0 and height == per_row * both
    assert both % 8 == 0 and height % 8 == 0 and pitch % 8 == 0

    def along(axis, size, target, value):
        return lax.ppermute(value, axis, [(i, target(i)) for i in range(size)])

    x = jnp.transpose(pair_rows, (1, 0, 2))
    far = [
        along("east", blocks, lambda e, s=s: (e + s * CORES) % blocks, x)
        for s in range(1, levels)
    ]
    beside = along("east", blocks, lambda e: e ^ 1, x)

    copied = (
        in_gain.reshape(1, channels),
        mid_gain.reshape(1, mix_width),
        left_weight,
        left_gate,
        right_weight,
        right_gate,
        out_weight,
    )
    n = len(copied)
    ready, gate, own_right, turn, gain, mid, lw, lg, rw, rg, ow = call(
        lambda *refs: own_kernel(n, pitch, *refs),
        (
            shape((pairs, channels)),
            shape((pairs, channels), F32),
            shape((pairs, mix_width), F32),
            shape((CORES, pairs, part_rows * pitch)),
            *(shape(a.shape, a.dtype) for a in copied),
        ),
        [HBM] * (2 + n),
        [pltpu.with_memory_space_constraint(a, pltpu.HBM) for a in (x, out_gate, *copied)],
        1.5,
        [
            pltpu.VMEM(x.shape, BF16),
            pltpu.VMEM(out_gate.shape, BF16),
            pltpu.SemaphoreType.DMA((2 + n,)),
        ],
    )

    part = shape((width, both, mix_width))
    flat = pltpu.VMEM((pairs, mix_width), F32)
    right, own_part = call(
        first_kernel,
        (shape((height, both // 8, 8, mix_width), F32), part),
        [VMEM] * 8,
        (beside, gain, lw, lg, rw, rg, ready, own_right),
        1.0,
        [pltpu.VMEM((both * height, mix_width), F32), flat],
    )
    parts = [own_part]
    for s in range(1, levels - 1):
        parts.append(
            call(next_kernel, part, [VMEM] * 5, (far[s - 1], gain, lw, lg, right), 0.6, [flat])
        )
    sums = call(
        lambda *refs: last_kernel(levels, rows, *refs),
        (shape((part_rows, both, mix_width)),) * rows,
        [VMEM] * (4 + levels),
        (far[-1], gain, lw, lg, right, *parts),
        0.8,
        [pltpu.VMEM((levels, width, both, mix_width), BF16), flat],
    )
    arrived = [sums[0]] + [
        along("north", rows, lambda n, a=a: n ^ a, sums[a]) for a in range(1, rows)
    ]

    half = shape((part_rows, pitch, mix_width))
    scale = (height * rows) ** (-0.5)
    keep, send = call(
        lambda *refs: sum_kernel(scale, *refs),
        (half, half),
        [VMEM] * (1 + rows),
        (mid, *arrived),
        0.3,
    )
    come = along("east", blocks, lambda e: e ^ 1, send)
    kept = call(keep_kernel, shape((pairs, channels), F32), [VMEM] * 3, (keep, turn, ow), 0.3)
    out = call(
        out_kernel, shape((width, height, channels)), [VMEM] * 5, (come, turn, ow, kept, gate), 0.5
    )
    return jnp.transpose(out, (1, 0, 2))


def solution(mesh):
    placed = (P("north", "east", None), P(), P(), P(), P(), P(), P(), P(), P())

    return jax.shard_map(
        body, mesh=mesh, in_specs=placed, out_specs=P("north", "east", None), check_vma=False
    )
```

profile of v0, /device:TPU:0, one launch (start us, length us, event | category | flops | bytes accessed | tf_op | source)
XLA Modules:
  0.0 23.5 jit_solution(3264929239969500737)
XLA Ops:
  0.0 0.5 %collective-permute-start.1 = (bf16[12,24,128]{2,1,0:T(8,128)(2,1)}, bf16[12,24,128]{2,1,0:T(8,128)(2,1)S(1)}, u32[]{:S(2)}, u32[]{:S(2)}) collective-permute-start(bf16[12,24,128]{2,1,0:T(8,128)(2,1)} %bitcast.4), channel_id=1, source_target_pairs={{0,1},{1,0},{2,3},{3,2},{4,5},{5,4},{6,7},{7,6},{8,9},{9,8},{10,11... | collective-permute-start | bytes 221192 | tf_op jit(solution)/shard_map/ppermute | solution.py:212
  0.5 3.6 %collective-permute-start.3 = (bf16[12,24,128]{2,1,0:T(8,128)(2,1)}, bf16[12,24,128]{2,1,0:T(8,128)(2,1)S(1)}, u32[]{:S(2)}, u32[]{:S(2)}) collective-permute-start(bf16[12,24,128]{2,1,0:T(8,128)(2,1)} %bitcast.5), channel_id=1, source_target_pairs={{0,4},{1,5},{2,6},{3,7},{4,0},{5,1},{6,2},{7,3},{8,12},{9,13},{10,... | collective-permute-start | bytes 221192 | tf_op jit(solution)/shard_map/ppermute | solution.py:212
  4.1 1.6 %collective-permute-start.2 = (bf16[12,24,128]{2,1,0:T(8,128)(2,1)}, bf16[12,24,128]{2,1,0:T(8,128)(2,1)S(1)}, u32[]{:S(2)}, u32[]{:S(2)}) collective-permute-start(bf16[12,24,128]{2,1,0:T(8,128)(2,1)} %bitcast.6), channel_id=1, source_target_pairs={{0,2},{1,3},{2,4},{3,5},{4,6},{5,7},{6,0},{7,1},{8,10},{9,11},{10,... | collective-permute-start | bytes 221192 | tf_op jit(solution)/shard_map/ppermute | solution.py:212
  5.6 2.2 %collective-permute-start = (bf16[12,24,128]{2,1,0:T(8,128)(2,1)}, bf16[12,24,128]{2,1,0:T(8,128)(2,1)S(1)}, u32[]{:S(2)}, u32[]{:S(2)}) collective-permute-start(bf16[12,24,128]{2,1,0:T(8,128)(2,1)} %bitcast.7), channel_id=1, source_target_pairs={{0,6},{1,7},{2,0},{3,1},{4,2},{5,3},{6,4},{7,5},{8,14},{9,15},{10,... | collective-permute-start | bytes 221192 | tf_op jit(solution)/shard_map/ppermute | solution.py:212
  7.9 1.4 %shard_map.91 = (bf16[288,128]{1,0:T(8,128)(2,1)S(1)}, f32[288,128]{1,0:T(8,128)S(1)}, f32[288,128]{1,0:T(8,128)S(1)}, bf16[2,288,192]{2,1,0:T(8,128)(2,1)S(1)},...) custom-call(bf16[12,24,128]{2,1,0:T(8,128)(2,1)} %bitcast.8, ...), custom_call_target="tpu_custom_call" | custom-call | flops 24000000 | tf_op jit(solution)/shard_map/pallas_call | solution.py:38
  9.3 0.0 collective-permute-done.1.x_ref
  9.3 0.7 %shard_map.92 = (f32[24,3,8,128]{3,2,1,0:T(8,128)S(1)}, bf16[12,24,128]{2,1,0:T(8,128)(2,1)S(1)}) custom-call(bf16[12,24,128]{2,1,0:T(8,128)(2,1)S(1)} %collective-permute-done.1.x_ref, f32[1,128]{1,0:T(1,128)S(1)} %get-tuple-element.25.gain_ref.refs_1_, bf16[128,128]{1,0:T(8,128)(2,1)S(1)} %get-tuple-element.26.lw_ref.refs_2_, ...), custom_call_target="tpu_custom_call" | custom-call | flops 16000000 | tf_op jit(solution)/shard_map/pallas_call | solution.py:38
  10.0 0.0 collective-permute-done.3.x_ref
  10.0 0.6 %shard_map.94.refs_7_ = bf16[12,24,128]{2,1,0:T(8,128)(2,1)S(1)} custom-call(bf16[12,24,128]{2,1,0:T(8,128)(2,1)S(1)} %collective-permute-done.3.x_ref, f32[1,128]{1,0:T(1,128)S(1)} %get-tuple-element.25.gain_ref.refs_1_, bf16[128,128]{1,0:T(8,128)(2,1)S(1)} %get-tuple-element.26.lw_ref.refs_2_, bf16[128,128]{1,0:T(8,128)(2,1)S(1)} %get-tuple-element.27.lg_ref.refs_3_, ...), custom_call_target="tpu_custom_call" | custom-call | flops 9600000 | tf_op jit(solution)/shard_map/pallas_call | solution.py:38
  10.6 0.6 %collective-permute-done.2.x_ref = bf16[12,24,128]{2,1,0:T(8,128)(2,1)S(1)} collective-permute-done((bf16[12,24,128]{2,1,0:T(8,128)(2,1)}, bf16[12,24,128]{2,1,0:T(8,128)(2,1)S(1)}, u32[]{:S(2)}, u32[]{:S(2)}) %collective-permute-start.2) | collective-permute-done | bytes 73760 | tf_op jit(solution)/shard_map/ppermute | solution.py:212
  11.2 0.6 %shard_map.93.refs_6_ = bf16[12,24,128]{2,1,0:T(8,128)(2,1)S(1)} custom-call(bf16[12,24,128]{2,1,0:T(8,128)(2,1)S(1)} %collective-permute-done.2.x_ref, f32[1,128]{1,0:T(1,128)S(1)} %get-tuple-element.25.gain_ref.refs_1_, bf16[128,128]{1,0:T(8,128)(2,1)S(1)} %get-tuple-element.26.lw_ref.refs_2_, bf16[128,128]{1,0:T(8,128)(2,1)S(1)} %get-tuple-element.27.lg_ref.refs_3_, ...), custom_call_target="tpu_custom_call" | custom-call | flops 9600000 | tf_op jit(solution)/shard_map/pallas_call | solution.py:38
  11.8 0.1 collective-permute-done.refs_0_
  12.0 0.6 %shard_map.95 = (bf16[12,24,128]{2,1,0:T(8,128)(2,1)S(1)}, bf16[12,24,128]{2,1,0:T(8,128)(2,1)S(1)}, bf16[12,24,128]{2,1,0:T(8,128)(2,1)S(1)}, bf16[12,24,128]{2,1,0:T(8,128)(2,1)S(1)}) custom-call(bf16[12,24,128]{2,1,0:T(8,128)(2,1)S(1)} %collective-permute-done.refs_0_, f32[1,128]{1,0:T(1,128)S(1)} %get-tuple-element.25.gain_ref.refs_1_, ...), custom_call_target="tpu_custom_call" | custom-call | flops 12800000 | tf_op jit(solution)/shard_map/pallas_call | solution.py:38
  12.6 1.6 %collective-permute-start.4 = (bf16[12,24,128]{2,1,0:T(8,128)(2,1)S(1)}, bf16[12,24,128]{2,1,0:T(8,128)(2,1)S(1)}, u32[]{:S(2)}, u32[]{:S(2)}) collective-permute-start(bf16[12,24,128]{2,1,0:T(8,128)(2,1)S(1)} %get-tuple-element.35), channel_id=1, source_target_pairs={{0,8},{8,0},{16,24},{24,16},{1,9},{9,1},{17,25},{25,17},{2,10},{10... | collective-permute-start | bytes 221192 | tf_op jit(solution)/shard_map/ppermute | solution.py:212
  14.2 1.5 %collective-permute-start.5 = (bf16[12,24,128]{2,1,0:T(8,128)(2,1)S(1)}, bf16[12,24,128]{2,1,0:T(8,128)(2,1)S(1)}, u32[]{:S(2)}, u32[]{:S(2)}) collective-permute-start(bf16[12,24,128]{2,1,0:T(8,128)(2,1)S(1)} %get-tuple-element.36), channel_id=1, source_target_pairs={{0,16},{8,24},{16,0},{24,8},{1,17},{9,25},{17,1},{25,9},{2,18},{10... | collective-permute-start | bytes 221192 | tf_op jit(solution)/shard_map/ppermute | solution.py:212
  15.7 0.4 %collective-permute-start.6 = (bf16[12,24,128]{2,1,0:T(8,128)(2,1)S(1)}, bf16[12,24,128]{2,1,0:T(8,128)(2,1)S(1)}, u32[]{:S(2)}, u32[]{:S(2)}) collective-permute-start(bf16[12,24,128]{2,1,0:T(8,128)(2,1)S(1)} %get-tuple-element.37), channel_id=1, source_target_pairs={{0,24},{8,16},{16,8},{24,0},{1,25},{9,17},{17,9},{25,1},{2,26},{10... | collective-permute-start | bytes 221192 | tf_op jit(solution)/shard_map/ppermute | solution.py:212
  16.2 0.9 %collective-permute-done.4.refs_2_ = bf16[12,24,128]{2,1,0:T(8,128)(2,1)S(1)} collective-permute-done((bf16[12,24,128]{2,1,0:T(8,128)(2,1)S(1)}, bf16[12,24,128]{2,1,0:T(8,128)(2,1)S(1)}, u32[]{:S(2)}, u32[]{:S(2)}) %collective-permute-start.4) | collective-permute-done | bytes 73760 | tf_op jit(solution)/shard_map/ppermute | solution.py:212
  17.0 2.3 %collective-permute-done.5.refs_3_ = bf16[12,24,128]{2,1,0:T(8,128)(2,1)S(1)} collective-permute-done((bf16[12,24,128]{2,1,0:T(8,128)(2,1)S(1)}, bf16[12,24,128]{2,1,0:T(8,128)(2,1)S(1)}, u32[]{:S(2)}, u32[]{:S(2)}) %collective-permute-start.5) | collective-permute-done | bytes 73760 | tf_op jit(solution)/shard_map/ppermute | solution.py:212
  19.4 1.6 %collective-permute-done.6.refs_4_ = bf16[12,24,128]{2,1,0:T(8,128)(2,1)S(1)} collective-permute-done((bf16[12,24,128]{2,1,0:T(8,128)(2,1)S(1)}, bf16[12,24,128]{2,1,0:T(8,128)(2,1)S(1)}, u32[]{:S(2)}, u32[]{:S(2)}) %collective-permute-start.6) | collective-permute-done | bytes 73760 | tf_op jit(solution)/shard_map/ppermute | solution.py:212
  21.0 0.2 shard_map.96
  21.2 0.1 collective-permute-start.7
  21.3 0.3 %shard_map.97.kept_ref = f32[288,128]{1,0:T(8,128)S(1)} custom-call(bf16[12,16,128]{2,1,0:T(8,128)(2,1)S(1)} %get-tuple-element.41.keep_ref, bf16[2,288,192]{2,1,0:T(8,128)(2,1)S(1)} %get-tuple-element.39.turn_ref, bf16[128,128]{1,0:T(8,128)(2,1)S(1)} %get-tuple-element.40.weight_ref), custom_call_target="tpu_custom_call" | custom-call | flops 4800000 | tf_op jit(solution)/shard_map/pallas_call | solution.py:38
  21.6 0.9 %collective-permute-done.7.come_ref = bf16[12,16,128]{2,1,0:T(8,128)(2,1)S(1)} collective-permute-done((bf16[12,16,128]{2,1,0:T(8,128)(2,1)S(1)}, bf16[12,16,128]{2,1,0:T(8,128)(2,1)S(1)}, u32[]{:S(2)}, u32[]{:S(2)}) %collective-permute-start.7) | collective-permute-done | bytes 49184 | tf_op jit(solution)/shard_map/ppermute | solution.py:212
  22.5 1.0 %shard_map.98 = bf16[12,24,128]{2,1,0:T(8,128)(2,1)} custom-call(bf16[12,16,128]{2,1,0:T(8,128)(2,1)S(1)} %collective-permute-done.7.come_ref, bf16[2,288,192]{2,1,0:T(8,128)(2,1)S(1)} %get-tuple-element.39.turn_ref, bf16[128,128]{1,0:T(8,128)(2,1)S(1)} %get-tuple-element.40.weight_ref, f32[288,128]{1,0:T(8,128)S(1)} %shard_map.97.kept_ref, ...), custom_call_target="tpu_custom_call" | custom-call | flops 8000000 | tf_op jit(solution)/shard_map/pallas_call | solution.py:38
Async XLA Ops:
  0.0 9.3 %collective-permute-start.1 = (bf16[12,24,128]{2,1,0:T(8,128)(2,1)}, bf16[12,24,128]{2,1,0:T(8,128)(2,1)S(1)}, u32[]{:S(2)}, u32[]{:S(2)}) collective-permute-start(bf16[12,24,128]{2,1,0:T(8,128)(2,1)} %bitcast.4), channel_id=1, source_target_pairs={{0,1},{1,0},{2,3},{3,2},{4,5},{5,4},{6,7},{7,6},{8,9},{9,8},{10,11... | collective-permute-start | bytes 221192 | tf_op jit(solution)/shard_map/ppermute | solution.py:212
  0.5 9.5 %collective-permute-start.3 = (bf16[12,24,128]{2,1,0:T(8,128)(2,1)}, bf16[12,24,128]{2,1,0:T(8,128)(2,1)S(1)}, u32[]{:S(2)}, u32[]{:S(2)}) collective-permute-start(bf16[12,24,128]{2,1,0:T(8,128)(2,1)} %bitcast.5), channel_id=1, source_target_pairs={{0,4},{1,5},{2,6},{3,7},{4,0},{5,1},{6,2},{7,3},{8,12},{9,13},{10,... | collective-permute-start | bytes 221192 | tf_op jit(solution)/shard_map/ppermute | solution.py:212
  4.1 7.2 %collective-permute-start.2 = (bf16[12,24,128]{2,1,0:T(8,128)(2,1)}, bf16[12,24,128]{2,1,0:T(8,128)(2,1)S(1)}, u32[]{:S(2)}, u32[]{:S(2)}) collective-permute-start(bf16[12,24,128]{2,1,0:T(8,128)(2,1)} %bitcast.6), channel_id=1, source_target_pairs={{0,2},{1,3},{2,4},{3,5},{4,6},{5,7},{6,0},{7,1},{8,10},{9,11},{10,... | collective-permute-start | bytes 221192 | tf_op jit(solution)/shard_map/ppermute | solution.py:212
  5.6 6.3 %collective-permute-start = (bf16[12,24,128]{2,1,0:T(8,128)(2,1)}, bf16[12,24,128]{2,1,0:T(8,128)(2,1)S(1)}, u32[]{:S(2)}, u32[]{:S(2)}) collective-permute-start(bf16[12,24,128]{2,1,0:T(8,128)(2,1)} %bitcast.7), channel_id=1, source_target_pairs={{0,6},{1,7},{2,0},{3,1},{4,2},{5,3},{6,4},{7,5},{8,14},{9,15},{10,... | collective-permute-start | bytes 221192 | tf_op jit(solution)/shard_map/ppermute | solution.py:212
  12.6 4.4 %collective-permute-start.4 = (bf16[12,24,128]{2,1,0:T(8,128)(2,1)S(1)}, bf16[12,24,128]{2,1,0:T(8,128)(2,1)S(1)}, u32[]{:S(2)}, u32[]{:S(2)}) collective-permute-start(bf16[12,24,128]{2,1,0:T(8,128)(2,1)S(1)} %get-tuple-element.35), channel_id=1, source_target_pairs={{0,8},{8,0},{16,24},{24,16},{1,9},{9,1},{17,25},{25,17},{2,10},{10... | collective-permute-start | bytes 221192 | tf_op jit(solution)/shard_map/ppermute | solution.py:212
  14.2 5.1 %collective-permute-start.5 = (bf16[12,24,128]{2,1,0:T(8,128)(2,1)S(1)}, bf16[12,24,128]{2,1,0:T(8,128)(2,1)S(1)}, u32[]{:S(2)}, u32[]{:S(2)}) collective-permute-start(bf16[12,24,128]{2,1,0:T(8,128)(2,1)S(1)} %get-tuple-element.36), channel_id=1, source_target_pairs={{0,16},{8,24},{16,0},{24,8},{1,17},{9,25},{17,1},{25,9},{2,18},{10... | collective-permute-start | bytes 221192 | tf_op jit(solution)/shard_map/ppermute | solution.py:212
  15.7 5.3 %collective-permute-start.6 = (bf16[12,24,128]{2,1,0:T(8,128)(2,1)S(1)}, bf16[12,24,128]{2,1,0:T(8,128)(2,1)S(1)}, u32[]{:S(2)}, u32[]{:S(2)}) collective-permute-start(bf16[12,24,128]{2,1,0:T(8,128)(2,1)S(1)} %get-tuple-element.37), channel_id=1, source_target_pairs={{0,24},{8,16},{16,8},{24,0},{1,25},{9,17},{17,9},{25,1},{2,26},{10... | collective-permute-start | bytes 221192 | tf_op jit(solution)/shard_map/ppermute | solution.py:212
  21.2 1.3 %collective-permute-start.7 = (bf16[12,16,128]{2,1,0:T(8,128)(2,1)S(1)}, bf16[12,16,128]{2,1,0:T(8,128)(2,1)S(1)}, u32[]{:S(2)}, u32[]{:S(2)}) collective-permute-start(bf16[12,16,128]{2,1,0:T(8,128)(2,1)S(1)} %get-tuple-element.38), channel_id=1, source_target_pairs={{0,1},{1,0},{2,3},{3,2},{4,5},{5,4},{6,7},{7,6},{8,9},{9,8},{10,11... | collective-permute-start | bytes 147464 | tf_op jit(solution)/shard_map/ppermute | solution.py:212
where the time goes:
time: 23.6 us; the launch traced here: 23.5 us
  starting transfers between devices  11.5 us (49%)
  waiting for transfers between devices  6.5 us (28%)
  Pallas kernels  5.37 us (23%)
    ppermute x8, starting transfers between devices, along(): return lax.ppermute(value, axis, [(i, target(i)) for i in range(size)])  11.5 us
    ppermute x8, waiting for transfers between devices, along(): return lax.ppermute(value, axis, [(i, target(i)) for i in range(size)])  6.5 us
    pallas_call x8, Pallas kernels, call(): pl.pallas_call(kernel, out_shape=outs, in_specs=specs, out_specs=tree, sc...  5.37 us
  transfers between devices with their start and end apart: 8, of which 6 were waited for; matrix products, arithmetic and copies ran while one was open for 0% of the time, Pallas kernels for 15%

commit v1 on v0

--- a/solution.py
+++ b/solution.py
@@ -141,7 +141,8 @@
     mix(part_ref, left_ref, right_ref)
 
 
-def last_kernel(levels, rows, *refs):
+def last_kernel(shifts, rows, *refs):
+    levels = len(shifts)
     x_ref, gain_ref, lw_ref, lg_ref, right_ref = refs[:5]
     parts = refs[5 : 4 + levels]
     outs = refs[4 + levels : 4 + levels + rows]
@@ -155,7 +156,8 @@
     width = all_ref.shape[1]
     for a, out_ref in enumerate(outs):
         for r in range(per_row):
-            s = lax.rem(level - ((row ^ a) * per_row + r) + levels, levels)
+            shift = level ^ ((row ^ a) * per_row + r)
+            s = sum(jnp.where(shift == v, at, 0) for at, v in enumerate(shifts))
             out_ref[pl.ds(r * width, width)] = all_ref[s]
 
 
@@ -205,16 +207,18 @@
     mix_width = left_weight.shape[1]
     both, pairs, part_rows = CORES * width, width * height, per_row * width
     pitch = both - width // 8 * 8
-    assert levels == per_row * rows and rows & (rows - 1) == 0 and height == per_row * both
+    assert levels == per_row * rows and levels & (levels - 1) == 0 and height == per_row * both
     assert both % 8 == 0 and height % 8 == 0 and pitch % 8 == 0
 
     def along(axis, size, target, value):
         return lax.ppermute(value, axis, [(i, target(i)) for i in range(size)])
 
+    shifts = (0, levels - 1, *range(1, levels - 1))
     x = jnp.transpose(pair_rows, (1, 0, 2))
     far = [
-        along("east", blocks, lambda e, s=s: (e + s * CORES) % blocks, x)
-        for s in range(1, levels)
+        along("east", blocks, lambda e, shift=shift: e ^ (shift * CORES), x)
+        for at, shift in enumerate(shifts)
+        if at
     ]
     beside = along("east", blocks, lambda e: e ^ 1, x)
 
@@ -263,7 +267,7 @@
             call(next_kernel, part, [VMEM] * 5, (far[s - 1], gain, lw, lg, right), 0.6, [flat])
         )
     sums = call(
-        lambda *refs: last_kernel(levels, rows, *refs),
+        lambda *refs: last_kernel(shifts, rows, *refs),
         (shape((part_rows, both, mix_width)),) * rows,
         [VMEM] * (4 + levels),
         (far[-1], gain, lw, lg, right, *parts),

time: 23.6 us -> 24.9 us (1.055)
  waiting for transfers between devices: 6.5 us -> 10 us
  starting transfers between devices: 11.5 us -> 9.27 us
    ppermute x8, waiting for transfers between devices: 6.5 us -> 10 us  [along(): return lax.ppermute(value, axis, [(i, target(i)) for i in range(size)])]
    ppermute x8, starting transfers between devices: 11.5 us -> 9.27 us  [along(): return lax.ppermute(value, axis, [(i, target(i)) for i in range(size)])]
  transfers between devices with their start and end apart: 8 -> 8, of which waited for: 6 -> 6; matrix products, arithmetic and copies ran while one was open for 0% -> 0% of each run, Pallas kernels for 15% -> 14%
where the time goes in v1:
time: 24.9 us; the launch traced here: 24.7 us
  waiting for transfers between devices  10 us (40%)
  starting transfers between devices  9.27 us (37%)
  Pallas kernels  5.36 us (22%)
    ppermute x8, waiting for transfers between devices, along(): return lax.ppermute(value, axis, [(i, target(i)) for i in range(size)])  10 us
    ppermute x8, starting transfers between devices, along(): return lax.ppermute(value, axis, [(i, target(i)) for i in range(size)])  9.27 us
    pallas_call x8, Pallas kernels, call(): pl.pallas_call(kernel, out_shape=outs, in_specs=specs, out_specs=tree, sc...  5.36 us
  transfers between devices with their start and end apart: 8, of which 6 were waited for; matrix products, arithmetic and copies ran while one was open for 0% of the time, Pallas kernels for 14%

profile of v1, /device:TPU:0, one launch (start us, length us, event | category | flops | bytes accessed | tf_op | source)
XLA Modules:
  0.0 24.7 jit_solution(6449662754405359892)
XLA Ops:
  0.0 0.5 %collective-permute-start.1 = (bf16[12,24,128]{2,1,0:T(8,128)(2,1)}, bf16[12,24,128]{2,1,0:T(8,128)(2,1)S(1)}, u32[]{:S(2)}, u32[]{:S(2)}) collective-permute-start(bf16[12,24,128]{2,1,0:T(8,128)(2,1)} %bitcast.4), channel_id=1, source_target_pairs={{0,1},{1,0},{2,3},{3,2},{4,5},{5,4},{6,7},{7,6},{8,9},{9,8},{10,11... | collective-permute-start | bytes 221192 | tf_op jit(solution)/shard_map/ppermute | solution.py:214
  0.5 2.6 %collective-permute-start.3 = (bf16[12,24,128]{2,1,0:T(8,128)(2,1)}, bf16[12,24,128]{2,1,0:T(8,128)(2,1)S(1)}, u32[]{:S(2)}, u32[]{:S(2)}) collective-permute-start(bf16[12,24,128]{2,1,0:T(8,128)(2,1)} %bitcast.5), channel_id=1, source_target_pairs={{0,2},{1,3},{2,0},{3,1},{4,6},{5,7},{6,4},{7,5},{8,10},{9,11},{10,... | collective-permute-start | bytes 221192 | tf_op jit(solution)/shard_map/ppermute | solution.py:214
  3.1 2.5 %collective-permute-start.2 = (bf16[12,24,128]{2,1,0:T(8,128)(2,1)}, bf16[12,24,128]{2,1,0:T(8,128)(2,1)S(1)}, u32[]{:S(2)}, u32[]{:S(2)}) collective-permute-start(bf16[12,24,128]{2,1,0:T(8,128)(2,1)} %bitcast.6), channel_id=1, source_target_pairs={{0,6},{1,7},{2,4},{3,5},{4,2},{5,3},{6,0},{7,1},{8,14},{9,15},{10,... | collective-permute-start | bytes 221192 | tf_op jit(solution)/shard_map/ppermute | solution.py:214
  5.5 0.1 collective-permute-start
  5.6 1.4 %shard_map.91 = (bf16[288,128]{1,0:T(8,128)(2,1)S(1)}, f32[288,128]{1,0:T(8,128)S(1)}, f32[288,128]{1,0:T(8,128)S(1)}, bf16[2,288,192]{2,1,0:T(8,128)(2,1)S(1)},...) custom-call(bf16[12,24,128]{2,1,0:T(8,128)(2,1)} %bitcast.8, ...), custom_call_target="tpu_custom_call" | custom-call | flops 24000000 | tf_op jit(solution)/shard_map/pallas_call | solution.py:38
  7.0 0.0 collective-permute-done.1.x_ref
  7.0 0.7 %shard_map.92 = (f32[24,3,8,128]{3,2,1,0:T(8,128)S(1)}, bf16[12,24,128]{2,1,0:T(8,128)(2,1)S(1)}) custom-call(bf16[12,24,128]{2,1,0:T(8,128)(2,1)S(1)} %collective-permute-done.1.x_ref, f32[1,128]{1,0:T(1,128)S(1)} %get-tuple-element.25.gain_ref.refs_1_, bf16[128,128]{1,0:T(8,128)(2,1)S(1)} %get-tuple-element.26.lw_ref.refs_2_, ...), custom_call_target="tpu_custom_call" | custom-call | flops 16000000 | tf_op jit(solution)/shard_map/pallas_call | solution.py:38
  7.7 0.0 collective-permute-done.3.x_ref
  7.7 0.6 %shard_map.94.refs_7_ = bf16[12,24,128]{2,1,0:T(8,128)(2,1)S(1)} custom-call(bf16[12,24,128]{2,1,0:T(8,128)(2,1)S(1)} %collective-permute-done.3.x_ref, f32[1,128]{1,0:T(1,128)S(1)} %get-tuple-element.25.gain_ref.refs_1_, bf16[128,128]{1,0:T(8,128)(2,1)S(1)} %get-tuple-element.26.lw_ref.refs_2_, bf16[128,128]{1,0:T(8,128)(2,1)S(1)} %get-tuple-element.27.lg_ref.refs_3_, ...), custom_call_target="tpu_custom_call" | custom-call | flops 9600000 | tf_op jit(solution)/shard_map/pallas_call | solution.py:38
  8.3 2.2 %collective-permute-done.2.x_ref = bf16[12,24,128]{2,1,0:T(8,128)(2,1)S(1)} collective-permute-done((bf16[12,24,128]{2,1,0:T(8,128)(2,1)}, bf16[12,24,128]{2,1,0:T(8,128)(2,1)S(1)}, u32[]{:S(2)}, u32[]{:S(2)}) %collective-permute-start.2) | collective-permute-done | bytes 73760 | tf_op jit(solution)/shard_map/ppermute | solution.py:214
  10.5 0.6 %shard_map.93.refs_6_ = bf16[12,24,128]{2,1,0:T(8,128)(2,1)S(1)} custom-call(bf16[12,24,128]{2,1,0:T(8,128)(2,1)S(1)} %collective-permute-done.2.x_ref, f32[1,128]{1,0:T(1,128)S(1)} %get-tuple-element.25.gain_ref.refs_1_, bf16[128,128]{1,0:T(8,128)(2,1)S(1)} %get-tuple-element.26.lw_ref.refs_2_, bf16[128,128]{1,0:T(8,128)(2,1)S(1)} %get-tuple-element.27.lg_ref.refs_3_, ...), custom_call_target="tpu_custom_call" | custom-call | flops 9600000 | tf_op jit(solution)/shard_map/pallas_call | solution.py:38
  11.1 2.1 %collective-permute-done.refs_0_ = bf16[12,24,128]{2,1,0:T(8,128)(2,1)S(1)} collective-permute-done((bf16[12,24,128]{2,1,0:T(8,128)(2,1)}, bf16[12,24,128]{2,1,0:T(8,128)(2,1)S(1)}, u32[]{:S(2)}, u32[]{:S(2)}) %collective-permute-start) | collective-permute-done | bytes 73760 | tf_op jit(solution)/shard_map/ppermute | solution.py:214
  13.3 0.6 %shard_map.95 = (bf16[12,24,128]{2,1,0:T(8,128)(2,1)S(1)}, bf16[12,24,128]{2,1,0:T(8,128)(2,1)S(1)}, bf16[12,24,128]{2,1,0:T(8,128)(2,1)S(1)}, bf16[12,24,128]{2,1,0:T(8,128)(2,1)S(1)}) custom-call(bf16[12,24,128]{2,1,0:T(8,128)(2,1)S(1)} %collective-permute-done.refs_0_, f32[1,128]{1,0:T(1,128)S(1)} %get-tuple-element.25.gain_ref.refs_1_, ...), custom_call_target="tpu_custom_call" | custom-call | flops 12800000 | tf_op jit(solution)/shard_map/pallas_call | solution.py:38
  13.9 1.6 %collective-permute-start.4 = (bf16[12,24,128]{2,1,0:T(8,128)(2,1)S(1)}, bf16[12,24,128]{2,1,0:T(8,128)(2,1)S(1)}, u32[]{:S(2)}, u32[]{:S(2)}) collective-permute-start(bf16[12,24,128]{2,1,0:T(8,128)(2,1)S(1)} %get-tuple-element.35), channel_id=1, source_target_pairs={{0,8},{8,0},{16,24},{24,16},{1,9},{9,1},{17,25},{25,17},{2,10},{10... | collective-permute-start | bytes 221192 | tf_op jit(solution)/shard_map/ppermute | solution.py:214
  15.5 1.5 %collective-permute-start.5 = (bf16[12,24,128]{2,1,0:T(8,128)(2,1)S(1)}, bf16[12,24,128]{2,1,0:T(8,128)(2,1)S(1)}, u32[]{:S(2)}, u32[]{:S(2)}) collective-permute-start(bf16[12,24,128]{2,1,0:T(8,128)(2,1)S(1)} %get-tuple-element.36), channel_id=1, source_target_pairs={{0,16},{8,24},{16,0},{24,8},{1,17},{9,25},{17,1},{25,9},{2,18},{10... | collective-permute-start | bytes 221192 | tf_op jit(solution)/shard_map/ppermute | solution.py:214
  17.0 0.5 %collective-permute-start.6 = (bf16[12,24,128]{2,1,0:T(8,128)(2,1)S(1)}, bf16[12,24,128]{2,1,0:T(8,128)(2,1)S(1)}, u32[]{:S(2)}, u32[]{:S(2)}) collective-permute-start(bf16[12,24,128]{2,1,0:T(8,128)(2,1)S(1)} %get-tuple-element.37), channel_id=1, source_target_pairs={{0,24},{8,16},{16,8},{24,0},{1,25},{9,17},{17,9},{25,1},{2,26},{10... | collective-permute-start | bytes 221192 | tf_op jit(solution)/shard_map/ppermute | solution.py:214
  17.5 0.9 %collective-permute-done.4.refs_2_ = bf16[12,24,128]{2,1,0:T(8,128)(2,1)S(1)} collective-permute-done((bf16[12,24,128]{2,1,0:T(8,128)(2,1)S(1)}, bf16[12,24,128]{2,1,0:T(8,128)(2,1)S(1)}, u32[]{:S(2)}, u32[]{:S(2)}) %collective-permute-start.4) | collective-permute-done | bytes 73760 | tf_op jit(solution)/shard_map/ppermute | solution.py:214
  18.3 1.5 %collective-permute-done.5.refs_3_ = bf16[12,24,128]{2,1,0:T(8,128)(2,1)S(1)} collective-permute-done((bf16[12,24,128]{2,1,0:T(8,128)(2,1)S(1)}, bf16[12,24,128]{2,1,0:T(8,128)(2,1)S(1)}, u32[]{:S(2)}, u32[]{:S(2)}) %collective-permute-start.5) | collective-permute-done | bytes 73760 | tf_op jit(solution)/shard_map/ppermute | solution.py:214
  19.8 2.4 %collective-permute-done.6.refs_4_ = bf16[12,24,128]{2,1,0:T(8,128)(2,1)S(1)} collective-permute-done((bf16[12,24,128]{2,1,0:T(8,128)(2,1)S(1)}, bf16[12,24,128]{2,1,0:T(8,128)(2,1)S(1)}, u32[]{:S(2)}, u32[]{:S(2)}) %collective-permute-start.6) | collective-permute-done | bytes 73760 | tf_op jit(solution)/shard_map/ppermute | solution.py:214
  22.3 0.2 shard_map.96
  22.5 0.1 collective-permute-start.7
  22.5 0.3 %shard_map.97.kept_ref = f32[288,128]{1,0:T(8,128)S(1)} custom-call(bf16[12,16,128]{2,1,0:T(8,128)(2,1)S(1)} %get-tuple-element.41.keep_ref, bf16[2,288,192]{2,1,0:T(8,128)(2,1)S(1)} %get-tuple-element.39.turn_ref, bf16[128,128]{1,0:T(8,128)(2,1)S(1)} %get-tuple-element.40.weight_ref), custom_call_target="tpu_custom_call" | custom-call | flops 4800000 | tf_op jit(solution)/shard_map/pallas_call | solution.py:38
  22.9 0.9 %collective-permute-done.7.come_ref = bf16[12,16,128]{2,1,0:T(8,128)(2,1)S(1)} collective-permute-done((bf16[12,16,128]{2,1,0:T(8,128)(2,1)S(1)}, bf16[12,16,128]{2,1,0:T(8,128)(2,1)S(1)}, u32[]{:S(2)}, u32[]{:S(2)}) %collective-permute-start.7) | collective-permute-done | bytes 49184 | tf_op jit(solution)/shard_map/ppermute | solution.py:214
  23.8 1.0 %shard_map.98 = bf16[12,24,128]{2,1,0:T(8,128)(2,1)} custom-call(bf16[12,16,128]{2,1,0:T(8,128)(2,1)S(1)} %collective-permute-done.7.come_ref, bf16[2,288,192]{2,1,0:T(8,128)(2,1)S(1)} %get-tuple-element.39.turn_ref, bf16[128,128]{1,0:T(8,128)(2,1)S(1)} %get-tuple-element.40.weight_ref, f32[288,128]{1,0:T(8,128)S(1)} %shard_map.97.kept_ref, ...), custom_call_target="tpu_custom_call" | custom-call | flops 8000000 | tf_op jit(solution)/shard_map/pallas_call | solution.py:38
Async XLA Ops:
  0.0 7.0 %collective-permute-start.1 = (bf16[12,24,128]{2,1,0:T(8,128)(2,1)}, bf16[12,24,128]{2,1,0:T(8,128)(2,1)S(1)}, u32[]{:S(2)}, u32[]{:S(2)}) collective-permute-start(bf16[12,24,128]{2,1,0:T(8,128)(2,1)} %bitcast.4), channel_id=1, source_target_pairs={{0,1},{1,0},{2,3},{3,2},{4,5},{5,4},{6,7},{7,6},{8,9},{9,8},{10,11... | collective-permute-start | bytes 221192 | tf_op jit(solution)/shard_map/ppermute | solution.py:214
  0.5 7.2 %collective-permute-start.3 = (bf16[12,24,128]{2,1,0:T(8,128)(2,1)}, bf16[12,24,128]{2,1,0:T(8,128)(2,1)S(1)}, u32[]{:S(2)}, u32[]{:S(2)}) collective-permute-start(bf16[12,24,128]{2,1,0:T(8,128)(2,1)} %bitcast.5), channel_id=1, source_target_pairs={{0,2},{1,3},{2,0},{3,1},{4,6},{5,7},{6,4},{7,5},{8,10},{9,11},{10,... | collective-permute-start | bytes 221192 | tf_op jit(solution)/shard_map/ppermute | solution.py:214
  3.1 7.5 %collective-permute-start.2 = (bf16[12,24,128]{2,1,0:T(8,128)(2,1)}, bf16[12,24,128]{2,1,0:T(8,128)(2,1)S(1)}, u32[]{:S(2)}, u32[]{:S(2)}) collective-permute-start(bf16[12,24,128]{2,1,0:T(8,128)(2,1)} %bitcast.6), channel_id=1, source_target_pairs={{0,6},{1,7},{2,4},{3,5},{4,2},{5,3},{6,0},{7,1},{8,14},{9,15},{10,... | collective-permute-start | bytes 221192 | tf_op jit(solution)/shard_map/ppermute | solution.py:214
  5.5 7.8 %collective-permute-start = (bf16[12,24,128]{2,1,0:T(8,128)(2,1)}, bf16[12,24,128]{2,1,0:T(8,128)(2,1)S(1)}, u32[]{:S(2)}, u32[]{:S(2)}) collective-permute-start(bf16[12,24,128]{2,1,0:T(8,128)(2,1)} %bitcast.7), channel_id=1, source_target_pairs={{0,4},{1,5},{2,6},{3,7},{4,0},{5,1},{6,2},{7,3},{8,12},{9,13},{10,... | collective-permute-start | bytes 221192 | tf_op jit(solution)/shard_map/ppermute | solution.py:214
  13.9 4.4 %collective-permute-start.4 = (bf16[12,24,128]{2,1,0:T(8,128)(2,1)S(1)}, bf16[12,24,128]{2,1,0:T(8,128)(2,1)S(1)}, u32[]{:S(2)}, u32[]{:S(2)}) collective-permute-start(bf16[12,24,128]{2,1,0:T(8,128)(2,1)S(1)} %get-tuple-element.35), channel_id=1, source_target_pairs={{0,8},{8,0},{16,24},{24,16},{1,9},{9,1},{17,25},{25,17},{2,10},{10... | collective-permute-start | bytes 221192 | tf_op jit(solution)/shard_map/ppermute | solution.py:214
  15.5 4.4 %collective-permute-start.5 = (bf16[12,24,128]{2,1,0:T(8,128)(2,1)S(1)}, bf16[12,24,128]{2,1,0:T(8,128)(2,1)S(1)}, u32[]{:S(2)}, u32[]{:S(2)}) collective-permute-start(bf16[12,24,128]{2,1,0:T(8,128)(2,1)S(1)} %get-tuple-element.36), channel_id=1, source_target_pairs={{0,16},{8,24},{16,0},{24,8},{1,17},{9,25},{17,1},{25,9},{2,18},{10... | collective-permute-start | bytes 221192 | tf_op jit(solution)/shard_map/ppermute | solution.py:214
  17.0 5.3 %collective-permute-start.6 = (bf16[12,24,128]{2,1,0:T(8,128)(2,1)S(1)}, bf16[12,24,128]{2,1,0:T(8,128)(2,1)S(1)}, u32[]{:S(2)}, u32[]{:S(2)}) collective-permute-start(bf16[12,24,128]{2,1,0:T(8,128)(2,1)S(1)} %get-tuple-element.37), channel_id=1, source_target_pairs={{0,24},{8,16},{16,8},{24,0},{1,25},{9,17},{17,9},{25,1},{2,26},{10... | collective-permute-start | bytes 221192 | tf_op jit(solution)/shard_map/ppermute | solution.py:214
  22.5 1.3 %collective-permute-start.7 = (bf16[12,16,128]{2,1,0:T(8,128)(2,1)S(1)}, bf16[12,16,128]{2,1,0:T(8,128)(2,1)S(1)}, u32[]{:S(2)}, u32[]{:S(2)}) collective-permute-start(bf16[12,16,128]{2,1,0:T(8,128)(2,1)S(1)} %get-tuple-element.38), channel_id=1, source_target_pairs={{0,1},{1,0},{2,3},{3,2},{4,5},{5,4},{6,7},{7,6},{8,9},{9,8},{10,11... | collective-permute-start | bytes 147464 | tf_op jit(solution)/shard_map/ppermute | solution.py:214

commit v2 on v1

--- a/solution.py
+++ b/solution.py
@@ -72,15 +72,17 @@
         move.start()
     width, height, _ = x_ref.shape
     columns = turn_ref.shape[2]
-    core = lax.rem(lax.axis_index("east"), CORES)
+    level, core = lax.div(lax.axis_index("east"), CORES), lax.rem(lax.axis_index("east"), CORES)
+    per_row = height // (CORES * width)
     row = lax.broadcasted_iota(jnp.int32, (height, columns), 0)
     column = lax.broadcasted_iota(jnp.int32, (height, columns), 1)
     for half in range(CORES):
         offset = half * (pitch - width)
-        at = core if half == 0 else 1 - core
         for j in range(width):
             hit = jnp.zeros((height, columns), F32)
-            for r in range(height // (CORES * width)):
+            for r in range(per_row):
+                near = level == lax.axis_index("north") * per_row + r
+                at = jnp.where(near, 1 - core, core) if half == 0 else jnp.where(near, core, 1 - core)
                 first = (r * CORES + at) * width
                 inside = (row >= first) & (row < first + width)
                 same = column == (row - first + r * width) * pitch + (j + offset)
@@ -127,9 +129,9 @@
 ):
     pairs = own_ref.shape[0]
     height, tiles_j, _, channels = right_ref.shape
-    flat_ref[pl.ds(0, pairs), :] = own_ref[...]
     other = gated(ready_of(x_ref, gain_ref[...]), rw_ref, rg_ref)
-    flat_ref[pl.ds(pairs, pairs), :] = other.astype(F32)
+    flat_ref[pl.ds(0, pairs), :] = other.astype(F32)
+    flat_ref[pl.ds(pairs, pairs), :] = own_ref[...]
     for k in range(height):
         right_ref[k] = flat_ref[pl.ds(k, tiles_j * 8, stride=height), :].reshape(tiles_j, 8, channels)
     left_ref[...] = gated(ready_ref[...], lw_ref, lg_ref).astype(F32)
@@ -213,10 +215,16 @@
     def along(axis, size, target, value):
         return lax.ppermute(value, axis, [(i, target(i)) for i in range(size)])
 
+    def across(target, value):
+        pairs = [
+            (n * blocks + e, target(n) * blocks + (e ^ 1)) for n in range(rows) for e in range(blocks)
+        ]
+        return lax.ppermute(value, ("north", "east"), pairs)
+
     shifts = (0, levels - 1, *range(1, levels - 1))
     x = jnp.transpose(pair_rows, (1, 0, 2))
     far = [
-        along("east", blocks, lambda e, shift=shift: e ^ (shift * CORES), x)
+        along("east", blocks, lambda e, shift=shift: e ^ (shift * CORES + 1), x)
         for at, shift in enumerate(shifts)
         if at
     ]
@@ -274,9 +282,8 @@
         0.8,
         [pltpu.VMEM((levels, width, both, mix_width), BF16), flat],
     )
-    arrived = [sums[0]] + [
-        along("north", rows, lambda n, a=a: n ^ a, sums[a]) for a in range(1, rows)
-    ]
+    own_sums = along("east", blocks, lambda e: e ^ 1, sums[0])
+    arrived = [own_sums] + [across(lambda n, a=a: n ^ a, sums[a]) for a in range(1, rows)]
 
     half = shape((part_rows, pitch, mix_width))
     scale = (height * rows) ** (-0.5)

time: 24.9 us -> 24.2 us (0.972)
  waiting for transfers between devices: 10 us -> 9.43 us
    ppermute x8 -> x6, waiting for transfers between devices: 10 us -> 5.02 us  [along(): return lax.ppermute(value, axis, [(i, target(i)) for i in range(size)])]
    ppermute x0 -> x3, waiting for transfers between devices: none -> 4.41 us  [across(): return lax.ppermute(value, ('north', 'east'), pairs)]
    ppermute x8 -> x6, starting transfers between devices: 9.27 us -> 6.01 us  [along(): return lax.ppermute(value, axis, [(i, target(i)) for i in range(size)])]
    ppermute x0 -> x3, starting transfers between devices: none -> 3.21 us  [across(): return lax.ppermute(value, ('north', 'east'), pairs)]
  transfers between devices with their start and end apart: 8 -> 9, of which waited for: 6 -> 6; matrix products, arithmetic and copies ran while one was open for 0% -> 0% of each run, Pallas kernels for 14% -> 15%
where the time goes in v2:
time: 24.2 us; the launch traced here: 24.1 us
  waiting for transfers between devices  9.43 us (39%)
  starting transfers between devices  9.22 us (38%)
  Pallas kernels  5.37 us (22%)
    ppermute x6, starting transfers between devices, along(): return lax.ppermute(value, axis, [(i, target(i)) for i in range(size)])  6.01 us
    pallas_call x8, Pallas kernels, call(): pl.pallas_call(kernel, out_shape=outs, in_specs=specs, out_specs=tree, sc...  5.37 us
    ppermute x6, waiting for transfers between devices, along(): return lax.ppermute(value, axis, [(i, target(i)) for i in range(size)])  5.02 us
    ppermute x3, waiting for transfers between devices, across(): return lax.ppermute(value, ('north', 'east'), pairs)  4.41 us
    ppermute x3, starting transfers between devices, across(): return lax.ppermute(value, ('north', 'east'), pairs)  3.21 us
  transfers between devices with their start and end apart: 9, of which 6 were waited for; matrix products, arithmetic and copies ran while one was open for 0% of the time, Pallas kernels for 15%

profile of v2, /device:TPU:0, one launch (start us, length us, event | category | flops | bytes accessed | tf_op | source)
XLA Modules:
  0.0 24.1 jit_solution(14377399668885696072)
XLA Ops:
  0.0 0.5 %collective-permute-start.1 = (bf16[12,24,128]{2,1,0:T(8,128)(2,1)}, bf16[12,24,128]{2,1,0:T(8,128)(2,1)S(1)}, u32[]{:S(2)}, u32[]{:S(2)}) collective-permute-start(bf16[12,24,128]{2,1,0:T(8,128)(2,1)} %bitcast.4), channel_id=1, source_target_pairs={{0,1},{1,0},{2,3},{3,2},{4,5},{5,4},{6,7},{7,6},{8,9},{9,8},{10,11... | collective-permute-start | bytes 221192 | tf_op jit(solution)/shard_map/ppermute | solution.py:216
  0.5 2.7 %collective-permute-start.3 = (bf16[12,24,128]{2,1,0:T(8,128)(2,1)}, bf16[12,24,128]{2,1,0:T(8,128)(2,1)S(1)}, u32[]{:S(2)}, u32[]{:S(2)}) collective-permute-start(bf16[12,24,128]{2,1,0:T(8,128)(2,1)} %bitcast.5), channel_id=1, source_target_pairs={{0,3},{1,2},{2,1},{3,0},{4,7},{5,6},{6,5},{7,4},{8,11},{9,10},{10,... | collective-permute-start | bytes 221192 | tf_op jit(solution)/shard_map/ppermute | solution.py:216
  3.2 2.1 %collective-permute-start.2 = (bf16[12,24,128]{2,1,0:T(8,128)(2,1)}, bf16[12,24,128]{2,1,0:T(8,128)(2,1)S(1)}, u32[]{:S(2)}, u32[]{:S(2)}) collective-permute-start(bf16[12,24,128]{2,1,0:T(8,128)(2,1)} %bitcast.6), channel_id=1, source_target_pairs={{0,7},{1,6},{2,5},{3,4},{4,3},{5,2},{6,1},{7,0},{8,15},{9,14},{10,... | collective-permute-start | bytes 221192 | tf_op jit(solution)/shard_map/ppermute | solution.py:216
  5.3 0.1 collective-permute-start
  5.4 1.4 %shard_map.91 = (bf16[288,128]{1,0:T(8,128)(2,1)S(1)}, f32[288,128]{1,0:T(8,128)S(1)}, f32[288,128]{1,0:T(8,128)S(1)}, bf16[2,288,192]{2,1,0:T(8,128)(2,1)S(1)},...) custom-call(bf16[12,24,128]{2,1,0:T(8,128)(2,1)} %bitcast.8, ...), custom_call_target="tpu_custom_call" | custom-call | flops 24000000 | tf_op jit(solution)/shard_map/pallas_call | solution.py:38
  6.8 0.0 collective-permute-done.1.x_ref
  6.8 0.7 %shard_map.92 = (f32[24,3,8,128]{3,2,1,0:T(8,128)S(1)}, bf16[12,24,128]{2,1,0:T(8,128)(2,1)S(1)}) custom-call(bf16[12,24,128]{2,1,0:T(8,128)(2,1)S(1)} %collective-permute-done.1.x_ref, f32[1,128]{1,0:T(1,128)S(1)} %get-tuple-element.25.gain_ref.refs_1_, bf16[128,128]{1,0:T(8,128)(2,1)S(1)} %get-tuple-element.26.lw_ref.refs_2_, ...), custom_call_target="tpu_custom_call" | custom-call | flops 16000000 | tf_op jit(solution)/shard_map/pallas_call | solution.py:38
  7.4 0.0 collective-permute-done.3.x_ref
  7.5 0.6 %shard_map.94.refs_7_ = bf16[12,24,128]{2,1,0:T(8,128)(2,1)S(1)} custom-call(bf16[12,24,128]{2,1,0:T(8,128)(2,1)S(1)} %collective-permute-done.3.x_ref, f32[1,128]{1,0:T(1,128)S(1)} %get-tuple-element.25.gain_ref.refs_1_, bf16[128,128]{1,0:T(8,128)(2,1)S(1)} %get-tuple-element.26.lw_ref.refs_2_, bf16[128,128]{1,0:T(8,128)(2,1)S(1)} %get-tuple-element.27.lg_ref.refs_3_, ...), custom_call_target="tpu_custom_call" | custom-call | flops 9600000 | tf_op jit(solution)/shard_map/pallas_call | solution.py:38
  8.1 1.8 %collective-permute-done.2.x_ref = bf16[12,24,128]{2,1,0:T(8,128)(2,1)S(1)} collective-permute-done((bf16[12,24,128]{2,1,0:T(8,128)(2,1)}, bf16[12,24,128]{2,1,0:T(8,128)(2,1)S(1)}, u32[]{:S(2)}, u32[]{:S(2)}) %collective-permute-start.2) | collective-permute-done | bytes 73760 | tf_op jit(solution)/shard_map/ppermute | solution.py:216
  9.8 0.6 %shard_map.93.refs_6_ = bf16[12,24,128]{2,1,0:T(8,128)(2,1)S(1)} custom-call(bf16[12,24,128]{2,1,0:T(8,128)(2,1)S(1)} %collective-permute-done.2.x_ref, f32[1,128]{1,0:T(1,128)S(1)} %get-tuple-element.25.gain_ref.refs_1_, bf16[128,128]{1,0:T(8,128)(2,1)S(1)} %get-tuple-element.26.lw_ref.refs_2_, bf16[128,128]{1,0:T(8,128)(2,1)S(1)} %get-tuple-element.27.lg_ref.refs_3_, ...), custom_call_target="tpu_custom_call" | custom-call | flops 9600000 | tf_op jit(solution)/shard_map/pallas_call | solution.py:38
  10.4 2.7 %collective-permute-done.refs_0_ = bf16[12,24,128]{2,1,0:T(8,128)(2,1)S(1)} collective-permute-done((bf16[12,24,128]{2,1,0:T(8,128)(2,1)}, bf16[12,24,128]{2,1,0:T(8,128)(2,1)S(1)}, u32[]{:S(2)}, u32[]{:S(2)}) %collective-permute-start) | collective-permute-done | bytes 73760 | tf_op jit(solution)/shard_map/ppermute | solution.py:216
  13.1 0.6 %shard_map.95 = (bf16[12,24,128]{2,1,0:T(8,128)(2,1)S(1)}, bf16[12,24,128]{2,1,0:T(8,128)(2,1)S(1)}, bf16[12,24,128]{2,1,0:T(8,128)(2,1)S(1)}, bf16[12,24,128]{2,1,0:T(8,128)(2,1)S(1)}) custom-call(bf16[12,24,128]{2,1,0:T(8,128)(2,1)S(1)} %collective-permute-done.refs_0_, f32[1,128]{1,0:T(1,128)S(1)} %get-tuple-element.25.gain_ref.refs_1_, ...), custom_call_target="tpu_custom_call" | custom-call | flops 12800000 | tf_op jit(solution)/shard_map/pallas_call | solution.py:38
  13.8 0.2 collective-permute-start.4
  13.9 1.5 %collective-permute-start.5 = (bf16[12,24,128]{2,1,0:T(8,128)(2,1)S(1)}, bf16[12,24,128]{2,1,0:T(8,128)(2,1)S(1)}, u32[]{:S(2)}, u32[]{:S(2)}) collective-permute-start(bf16[12,24,128]{2,1,0:T(8,128)(2,1)S(1)} %get-tuple-element.35), channel_id=1, source_target_pairs={{0,9},{1,8},{2,11},{3,10},{4,13},{5,12},{6,15},{7,14},{8,1},{9,0},... | collective-permute-start | bytes 221192 | tf_op jit(solution)/shard_map/ppermute | solution.py:222
  15.4 1.2 %collective-permute-start.6 = (bf16[12,24,128]{2,1,0:T(8,128)(2,1)S(1)}, bf16[12,24,128]{2,1,0:T(8,128)(2,1)S(1)}, u32[]{:S(2)}, u32[]{:S(2)}) collective-permute-start(bf16[12,24,128]{2,1,0:T(8,128)(2,1)S(1)} %get-tuple-element.36), channel_id=1, source_target_pairs={{0,17},{1,16},{2,19},{3,18},{4,21},{5,20},{6,23},{7,22},{8,25},{9,... | collective-permute-start | bytes 221192 | tf_op jit(solution)/shard_map/ppermute | solution.py:222
  16.7 0.5 %collective-permute-start.7 = (bf16[12,24,128]{2,1,0:T(8,128)(2,1)S(1)}, bf16[12,24,128]{2,1,0:T(8,128)(2,1)S(1)}, u32[]{:S(2)}, u32[]{:S(2)}) collective-permute-start(bf16[12,24,128]{2,1,0:T(8,128)(2,1)S(1)} %get-tuple-element.37), channel_id=1, source_target_pairs={{0,25},{1,24},{2,27},{3,26},{4,29},{5,28},{6,31},{7,30},{8,17},{9,... | collective-permute-start | bytes 221192 | tf_op jit(solution)/shard_map/ppermute | solution.py:222
  17.1 0.0 collective-permute-done.4.refs_1_
  17.1 0.8 %collective-permute-done.5.refs_2_ = bf16[12,24,128]{2,1,0:T(8,128)(2,1)S(1)} collective-permute-done((bf16[12,24,128]{2,1,0:T(8,128)(2,1)S(1)}, bf16[12,24,128]{2,1,0:T(8,128)(2,1)S(1)}, u32[]{:S(2)}, u32[]{:S(2)}) %collective-permute-start.5) | collective-permute-done | bytes 73760 | tf_op jit(solution)/shard_map/ppermute | solution.py:222
  17.9 2.7 %collective-permute-done.6.refs_3_ = bf16[12,24,128]{2,1,0:T(8,128)(2,1)S(1)} collective-permute-done((bf16[12,24,128]{2,1,0:T(8,128)(2,1)S(1)}, bf16[12,24,128]{2,1,0:T(8,128)(2,1)S(1)}, u32[]{:S(2)}, u32[]{:S(2)}) %collective-permute-start.6) | collective-permute-done | bytes 73760 | tf_op jit(solution)/shard_map/ppermute | solution.py:222
  20.6 0.9 %collective-permute-done.7.refs_4_ = bf16[12,24,128]{2,1,0:T(8,128)(2,1)S(1)} collective-permute-done((bf16[12,24,128]{2,1,0:T(8,128)(2,1)S(1)}, bf16[12,24,128]{2,1,0:T(8,128)(2,1)S(1)}, u32[]{:S(2)}, u32[]{:S(2)}) %collective-permute-start.7) | collective-permute-done | bytes 73760 | tf_op jit(solution)/shard_map/ppermute | solution.py:222
  21.6 0.2 shard_map.96
  21.8 0.5 %collective-permute-start.8 = (bf16[12,16,128]{2,1,0:T(8,128)(2,1)S(1)}, bf16[12,16,128]{2,1,0:T(8,128)(2,1)S(1)}, u32[]{:S(2)}, u32[]{:S(2)}) collective-permute-start(bf16[12,16,128]{2,1,0:T(8,128)(2,1)S(1)} %get-tuple-element.38), channel_id=1, source_target_pairs={{0,1},{1,0},{2,3},{3,2},{4,5},{5,4},{6,7},{7,6},{8,9},{9,8},{10,11... | collective-permute-start | bytes 147464 | tf_op jit(solution)/shard_map/ppermute | solution.py:216
  22.2 0.3 %shard_map.97.kept_ref = f32[288,128]{1,0:T(8,128)S(1)} custom-call(bf16[12,16,128]{2,1,0:T(8,128)(2,1)S(1)} %get-tuple-element.41.keep_ref, bf16[2,288,192]{2,1,0:T(8,128)(2,1)S(1)} %get-tuple-element.39.turn_ref, bf16[128,128]{1,0:T(8,128)(2,1)S(1)} %get-tuple-element.40.weight_ref), custom_call_target="tpu_custom_call" | custom-call | flops 4800000 | tf_op jit(solution)/shard_map/pallas_call | solution.py:38
  22.6 0.6 %collective-permute-done.8.come_ref = bf16[12,16,128]{2,1,0:T(8,128)(2,1)S(1)} collective-permute-done((bf16[12,16,128]{2,1,0:T(8,128)(2,1)S(1)}, bf16[12,16,128]{2,1,0:T(8,128)(2,1)S(1)}, u32[]{:S(2)}, u32[]{:S(2)}) %collective-permute-start.8) | collective-permute-done | bytes 49184 | tf_op jit(solution)/shard_map/ppermute | solution.py:216
  23.1 1.0 %shard_map.98 = bf16[12,24,128]{2,1,0:T(8,128)(2,1)} custom-call(bf16[12,16,128]{2,1,0:T(8,128)(2,1)S(1)} %collective-permute-done.8.come_ref, bf16[2,288,192]{2,1,0:T(8,128)(2,1)S(1)} %get-tuple-element.39.turn_ref, bf16[128,128]{1,0:T(8,128)(2,1)S(1)} %get-tuple-element.40.weight_ref, f32[288,128]{1,0:T(8,128)S(1)} %shard_map.97.kept_ref, ...), custom_call_target="tpu_custom_call" | custom-call | flops 8000000 | tf_op jit(solution)/shard_map/pallas_call | solution.py:38
Async XLA Ops:
  0.0 6.8 %collective-permute-start.1 = (bf16[12,24,128]{2,1,0:T(8,128)(2,1)}, bf16[12,24,128]{2,1,0:T(8,128)(2,1)S(1)}, u32[]{:S(2)}, u32[]{:S(2)}) collective-permute-start(bf16[12,24,128]{2,1,0:T(8,128)(2,1)} %bitcast.4), channel_id=1, source_target_pairs={{0,1},{1,0},{2,3},{3,2},{4,5},{5,4},{6,7},{7,6},{8,9},{9,8},{10,11... | collective-permute-start | bytes 221192 | tf_op jit(solution)/shard_map/ppermute | solution.py:216
  0.5 7.0 %collective-permute-start.3 = (bf16[12,24,128]{2,1,0:T(8,128)(2,1)}, bf16[12,24,128]{2,1,0:T(8,128)(2,1)S(1)}, u32[]{:S(2)}, u32[]{:S(2)}) collective-permute-start(bf16[12,24,128]{2,1,0:T(8,128)(2,1)} %bitcast.5), channel_id=1, source_target_pairs={{0,3},{1,2},{2,1},{3,0},{4,7},{5,6},{6,5},{7,4},{8,11},{9,10},{10,... | collective-permute-start | bytes 221192 | tf_op jit(solution)/shard_map/ppermute | solution.py:216
  3.2 6.7 %collective-permute-start.2 = (bf16[12,24,128]{2,1,0:T(8,128)(2,1)}, bf16[12,24,128]{2,1,0:T(8,128)(2,1)S(1)}, u32[]{:S(2)}, u32[]{:S(2)}) collective-permute-start(bf16[12,24,128]{2,1,0:T(8,128)(2,1)} %bitcast.6), channel_id=1, source_target_pairs={{0,7},{1,6},{2,5},{3,4},{4,3},{5,2},{6,1},{7,0},{8,15},{9,14},{10,... | collective-permute-start | bytes 221192 | tf_op jit(solution)/shard_map/ppermute | solution.py:216
  5.3 7.9 %collective-permute-start = (bf16[12,24,128]{2,1,0:T(8,128)(2,1)}, bf16[12,24,128]{2,1,0:T(8,128)(2,1)S(1)}, u32[]{:S(2)}, u32[]{:S(2)}) collective-permute-start(bf16[12,24,128]{2,1,0:T(8,128)(2,1)} %bitcast.7), channel_id=1, source_target_pairs={{0,5},{1,4},{2,7},{3,6},{4,1},{5,0},{6,3},{7,2},{8,13},{9,12},{10,... | collective-permute-start | bytes 221192 | tf_op jit(solution)/shard_map/ppermute | solution.py:216
  13.8 3.4 %collective-permute-start.4 = (bf16[12,24,128]{2,1,0:T(8,128)(2,1)S(1)}, bf16[12,24,128]{2,1,0:T(8,128)(2,1)S(1)}, u32[]{:S(2)}, u32[]{:S(2)}) collective-permute-start(bf16[12,24,128]{2,1,0:T(8,128)(2,1)S(1)} %get-tuple-element.34), channel_id=1, source_target_pairs={{0,1},{1,0},{2,3},{3,2},{4,5},{5,4},{6,7},{7,6},{8,9},{9,8},{10,11... | collective-permute-start | bytes 221192 | tf_op jit(solution)/shard_map/ppermute | solution.py:216
  13.9 4.0 %collective-permute-start.5 = (bf16[12,24,128]{2,1,0:T(8,128)(2,1)S(1)}, bf16[12,24,128]{2,1,0:T(8,128)(2,1)S(1)}, u32[]{:S(2)}, u32[]{:S(2)}) collective-permute-start(bf16[12,24,128]{2,1,0:T(8,128)(2,1)S(1)} %get-tuple-element.35), channel_id=1, source_target_pairs={{0,9},{1,8},{2,11},{3,10},{4,13},{5,12},{6,15},{7,14},{8,1},{9,0},... | collective-permute-start | bytes 221192 | tf_op jit(solution)/shard_map/ppermute | solution.py:222
  15.4 5.2 %collective-permute-start.6 = (bf16[12,24,128]{2,1,0:T(8,128)(2,1)S(1)}, bf16[12,24,128]{2,1,0:T(8,128)(2,1)S(1)}, u32[]{:S(2)}, u32[]{:S(2)}) collective-permute-start(bf16[12,24,128]{2,1,0:T(8,128)(2,1)S(1)} %get-tuple-element.36), channel_id=1, source_target_pairs={{0,17},{1,16},{2,19},{3,18},{4,21},{5,20},{6,23},{7,22},{8,25},{9,... | collective-permute-start | bytes 221192 | tf_op jit(solution)/shard_map/ppermute | solution.py:222
  16.7 4.9 %collective-permute-start.7 = (bf16[12,24,128]{2,1,0:T(8,128)(2,1)S(1)}, bf16[12,24,128]{2,1,0:T(8,128)(2,1)S(1)}, u32[]{:S(2)}, u32[]{:S(2)}) collective-permute-start(bf16[12,24,128]{2,1,0:T(8,128)(2,1)S(1)} %get-tuple-element.37), channel_id=1, source_target_pairs={{0,25},{1,24},{2,27},{3,26},{4,29},{5,28},{6,31},{7,30},{8,17},{9,... | collective-permute-start | bytes 221192 | tf_op jit(solution)/shard_map/ppermute | solution.py:222
  21.8 1.3 %collective-permute-start.8 = (bf16[12,16,128]{2,1,0:T(8,128)(2,1)S(1)}, bf16[12,16,128]{2,1,0:T(8,128)(2,1)S(1)}, u32[]{:S(2)}, u32[]{:S(2)}) collective-permute-start(bf16[12,16,128]{2,1,0:T(8,128)(2,1)S(1)} %get-tuple-element.38), channel_id=1, source_target_pairs={{0,1},{1,0},{2,3},{3,2},{4,5},{5,4},{6,7},{7,6},{8,9},{9,8},{10,11... | collective-permute-start | bytes 147464 | tf_op jit(solution)/shard_map/ppermute | solution.py:216

commit v3 on v0

--- a/solution.py
+++ b/solution.py
@@ -72,15 +72,17 @@
         move.start()
     width, height, _ = x_ref.shape
     columns = turn_ref.shape[2]
-    core = lax.rem(lax.axis_index("east"), CORES)
+    level, core = lax.div(lax.axis_index("east"), CORES), lax.rem(lax.axis_index("east"), CORES)
+    per_row = height // (CORES * width)
     row = lax.broadcasted_iota(jnp.int32, (height, columns), 0)
     column = lax.broadcasted_iota(jnp.int32, (height, columns), 1)
     for half in range(CORES):
         offset = half * (pitch - width)
-        at = core if half == 0 else 1 - core
         for j in range(width):
             hit = jnp.zeros((height, columns), F32)
-            for r in range(height // (CORES * width)):
+            for r in range(per_row):
+                near = level == lax.axis_index("north") * per_row + r
+                at = jnp.where(near, 1 - core, core) if half == 0 else jnp.where(near, core, 1 - core)
                 first = (r * CORES + at) * width
                 inside = (row >= first) & (row < first + width)
                 same = column == (row - first + r * width) * pitch + (j + offset)
@@ -127,9 +129,9 @@
 ):
     pairs = own_ref.shape[0]
     height, tiles_j, _, channels = right_ref.shape
-    flat_ref[pl.ds(0, pairs), :] = own_ref[...]
     other = gated(ready_of(x_ref, gain_ref[...]), rw_ref, rg_ref)
-    flat_ref[pl.ds(pairs, pairs), :] = other.astype(F32)
+    flat_ref[pl.ds(0, pairs), :] = other.astype(F32)
+    flat_ref[pl.ds(pairs, pairs), :] = own_ref[...]
     for k in range(height):
         right_ref[k] = flat_ref[pl.ds(k, tiles_j * 8, stride=height), :].reshape(tiles_j, 8, channels)
     left_ref[...] = gated(ready_ref[...], lw_ref, lg_ref).astype(F32)
@@ -139,6 +141,13 @@
 def next_kernel(x_ref, gain_ref, lw_ref, lg_ref, right_ref, part_ref, left_ref):
     left_ref[...] = gated(ready_of(x_ref, gain_ref[...]), lw_ref, lg_ref).astype(F32)
     mix(part_ref, left_ref, right_ref)
+
+
+def step_between(level, target, levels):
+    def place(z):
+        return lax.div(z, 2) + lax.rem(z, 2) * (levels // 2)
+
+    return lax.rem(place(target) - place(level) + levels, levels)
 
 
 def last_kernel(levels, rows, *refs):
@@ -155,7 +164,7 @@
     width = all_ref.shape[1]
     for a, out_ref in enumerate(outs):
         for r in range(per_row):
-            s = lax.rem(level - ((row ^ a) * per_row + r) + levels, levels)
+            s = step_between(level, (row ^ a) * per_row + r, levels)
             out_ref[pl.ds(r * width, width)] = all_ref[s]
 
 
@@ -205,18 +214,32 @@
     mix_width = left_weight.shape[1]
     both, pairs, part_rows = CORES * width, width * height, per_row * width
     pitch = both - width // 8 * 8
-    assert levels == per_row * rows and rows & (rows - 1) == 0 and height == per_row * both
+    assert levels == per_row * rows and rows & (rows - 1) == 0 and levels % 2 == 0 and height == per_row * both
     assert both % 8 == 0 and height % 8 == 0 and pitch % 8 == 0
 
-    def along(axis, size, target, value):
-        return lax.ppermute(value, axis, [(i, target(i)) for i in range(size)])
+    def along(axes, moves, value):
+        return lax.ppermute(value, axes, moves)
+
+    cores = [(e, e ^ 1) for e in range(blocks)]
+
+    circle = [*range(0, levels, 2), *range(1, levels, 2)]
+
+    def source(level, s):
+        return circle[(circle.index(level) + s) % levels]
 
     x = jnp.transpose(pair_rows, (1, 0, 2))
     far = [
-        along("east", blocks, lambda e, s=s: (e + s * CORES) % blocks, x)
+        along(
+            "east",
+            [
+                (source(e // CORES, s) * CORES + (1 - e % CORES), e)
+                for e in range(blocks)
+            ],
+            x,
+        )
         for s in range(1, levels)
     ]
-    beside = along("east", blocks, lambda e: e ^ 1, x)
+    beside = along("east", cores, x)
 
     copied = (
         in_gain.reshape(1, channels),
@@ -270,9 +293,12 @@
         0.8,
         [pltpu.VMEM((levels, width, both, mix_width), BF16), flat],
     )
-    arrived = [sums[0]] + [
-        along("north", rows, lambda n, a=a: n ^ a, sums[a]) for a in range(1, rows)
-    ]
+    arrived = [along("east", cores, sums[0])]
+    for a in range(1, rows):
+        moves = [
+            (n * blocks + e, (n ^ a) * blocks + (e ^ 1)) for n in range(rows) for e in range(blocks)
+        ]
+        arrived.append(along(("north", "east"), moves, sums[a]))
 
     half = shape((part_rows, pitch, mix_width))
     scale = (height * rows) ** (-0.5)
@@ -283,7 +309,7 @@
         (mid, *arrived),
         0.3,
     )
-    come = along("east", blocks, lambda e: e ^ 1, send)
+    come = along("east", cores, send)
     kept = call(keep_kernel, shape((pairs, channels), F32), [VMEM] * 3, (keep, turn, ow), 0.3)
     out = call(
         out_kernel, shape((width, height, channels)), [VMEM] * 5, (come, turn, ow, kept, gate), 0.5

time: 23.6 us -> 24 us (1.017)
  waiting for transfers between devices: 6.5 us -> 7.88 us
  starting transfers between devices: 11.5 us -> 10.5 us
    ppermute x8 -> x9, waiting for transfers between devices: 6.5 us -> 7.88 us  [along(): return lax.ppermute(value, axes, moves)]
    ppermute x8 -> x9, starting transfers between devices: 11.5 us -> 10.5 us  [along(): return lax.ppermute(value, axes, moves)]
  transfers between devices with their start and end apart: 8 -> 9, of which waited for: 6 -> 6; matrix products, arithmetic and copies ran while one was open for 0% -> 0% of each run, Pallas kernels for 15% -> 15%
where the time goes in v3:
time: 24 us; the launch traced here: 23.8 us
  starting transfers between devices  10.5 us (44%)
  waiting for transfers between devices  7.88 us (33%)
  Pallas kernels  5.37 us (22%)
    ppermute x9, starting transfers between devices, along(): return lax.ppermute(value, axes, moves)  10.5 us
    ppermute x9, waiting for transfers between devices, along(): return lax.ppermute(value, axes, moves)  7.88 us
    pallas_call x8, Pallas kernels, call(): pl.pallas_call(kernel, out_shape=outs, in_specs=specs, out_specs=tree, sc...  5.37 us
  transfers between devices with their start and end apart: 9, of which 6 were waited for; matrix products, arithmetic and copies ran while one was open for 0% of the time, Pallas kernels for 15%

profile of v3, /device:TPU:0, one launch (start us, length us, event | category | flops | bytes accessed | tf_op | source)
XLA Modules:
  0.0 23.8 jit_solution(12032207025455994982)
XLA Ops:
  0.0 0.5 %collective-permute-start.1 = (bf16[12,24,128]{2,1,0:T(8,128)(2,1)}, bf16[12,24,128]{2,1,0:T(8,128)(2,1)S(1)}, u32[]{:S(2)}, u32[]{:S(2)}) collective-permute-start(bf16[12,24,128]{2,1,0:T(8,128)(2,1)} %bitcast.4), channel_id=1, source_target_pairs={{0,1},{1,0},{2,3},{3,2},{4,5},{5,4},{6,7},{7,6},{8,9},{9,8},{10,11... | collective-permute-start | bytes 221192 | tf_op jit(solution)/shard_map/ppermute | solution.py:221
  0.5 2.7 %collective-permute-start.3 = (bf16[12,24,128]{2,1,0:T(8,128)(2,1)}, bf16[12,24,128]{2,1,0:T(8,128)(2,1)S(1)}, u32[]{:S(2)}, u32[]{:S(2)}) collective-permute-start(bf16[12,24,128]{2,1,0:T(8,128)(2,1)} %bitcast.5), channel_id=1, source_target_pairs={{3,0},{2,1},{1,2},{0,3},{7,4},{6,5},{5,6},{4,7},{11,8},{10,9},{9,1... | collective-permute-start | bytes 221192 | tf_op jit(solution)/shard_map/ppermute | solution.py:221
  3.2 2.1 %collective-permute-start.2 = (bf16[12,24,128]{2,1,0:T(8,128)(2,1)}, bf16[12,24,128]{2,1,0:T(8,128)(2,1)S(1)}, u32[]{:S(2)}, u32[]{:S(2)}) collective-permute-start(bf16[12,24,128]{2,1,0:T(8,128)(2,1)} %bitcast.6), channel_id=1, source_target_pairs={{5,0},{4,1},{7,2},{6,3},{3,4},{2,5},{1,6},{0,7},{13,8},{12,9},{15,... | collective-permute-start | bytes 221192 | tf_op jit(solution)/shard_map/ppermute | solution.py:221
  5.3 0.6 %collective-permute-start = (bf16[12,24,128]{2,1,0:T(8,128)(2,1)}, bf16[12,24,128]{2,1,0:T(8,128)(2,1)S(1)}, u32[]{:S(2)}, u32[]{:S(2)}) collective-permute-start(bf16[12,24,128]{2,1,0:T(8,128)(2,1)} %bitcast.7), channel_id=1, source_target_pairs={{7,0},{6,1},{5,2},{4,3},{1,4},{0,5},{3,6},{2,7},{15,8},{14,9},{13,... | collective-permute-start | bytes 221192 | tf_op jit(solution)/shard_map/ppermute | solution.py:221
  5.8 1.4 %shard_map.91 = (bf16[288,128]{1,0:T(8,128)(2,1)S(1)}, f32[288,128]{1,0:T(8,128)S(1)}, f32[288,128]{1,0:T(8,128)S(1)}, bf16[2,288,192]{2,1,0:T(8,128)(2,1)S(1)},...) custom-call(bf16[12,24,128]{2,1,0:T(8,128)(2,1)} %bitcast.8, ...), custom_call_target="tpu_custom_call" | custom-call | flops 24000000 | tf_op jit(solution)/shard_map/pallas_call | solution.py:38
  7.2 0.0 collective-permute-done.1.x_ref
  7.2 0.7 %shard_map.92 = (f32[24,3,8,128]{3,2,1,0:T(8,128)S(1)}, bf16[12,24,128]{2,1,0:T(8,128)(2,1)S(1)}) custom-call(bf16[12,24,128]{2,1,0:T(8,128)(2,1)S(1)} %collective-permute-done.1.x_ref, f32[1,128]{1,0:T(1,128)S(1)} %get-tuple-element.25.gain_ref.refs_1_, bf16[128,128]{1,0:T(8,128)(2,1)S(1)} %get-tuple-element.26.lw_ref.refs_2_, ...), custom_call_target="tpu_custom_call" | custom-call | flops 16000000 | tf_op jit(solution)/shard_map/pallas_call | solution.py:38
  7.9 0.0 collective-permute-done.3.x_ref
  7.9 0.6 %shard_map.94.refs_7_ = bf16[12,24,128]{2,1,0:T(8,128)(2,1)S(1)} custom-call(bf16[12,24,128]{2,1,0:T(8,128)(2,1)S(1)} %collective-permute-done.3.x_ref, f32[1,128]{1,0:T(1,128)S(1)} %get-tuple-element.25.gain_ref.refs_1_, bf16[128,128]{1,0:T(8,128)(2,1)S(1)} %get-tuple-element.26.lw_ref.refs_2_, bf16[128,128]{1,0:T(8,128)(2,1)S(1)} %get-tuple-element.27.lg_ref.refs_3_, ...), custom_call_target="tpu_custom_call" | custom-call | flops 9600000 | tf_op jit(solution)/shard_map/pallas_call | solution.py:38
  8.5 1.7 %collective-permute-done.2.x_ref = bf16[12,24,128]{2,1,0:T(8,128)(2,1)S(1)} collective-permute-done((bf16[12,24,128]{2,1,0:T(8,128)(2,1)}, bf16[12,24,128]{2,1,0:T(8,128)(2,1)S(1)}, u32[]{:S(2)}, u32[]{:S(2)}) %collective-permute-start.2) | collective-permute-done | bytes 73760 | tf_op jit(solution)/shard_map/ppermute | solution.py:221
  10.2 0.6 %shard_map.93.refs_6_ = bf16[12,24,128]{2,1,0:T(8,128)(2,1)S(1)} custom-call(bf16[12,24,128]{2,1,0:T(8,128)(2,1)S(1)} %collective-permute-done.2.x_ref, f32[1,128]{1,0:T(1,128)S(1)} %get-tuple-element.25.gain_ref.refs_1_, bf16[128,128]{1,0:T(8,128)(2,1)S(1)} %get-tuple-element.26.lw_ref.refs_2_, bf16[128,128]{1,0:T(8,128)(2,1)S(1)} %get-tuple-element.27.lg_ref.refs_3_, ...), custom_call_target="tpu_custom_call" | custom-call | flops 9600000 | tf_op jit(solution)/shard_map/pallas_call | solution.py:38
  10.8 0.4 %collective-permute-done.refs_0_ = bf16[12,24,128]{2,1,0:T(8,128)(2,1)S(1)} collective-permute-done((bf16[12,24,128]{2,1,0:T(8,128)(2,1)}, bf16[12,24,128]{2,1,0:T(8,128)(2,1)S(1)}, u32[]{:S(2)}, u32[]{:S(2)}) %collective-permute-start) | collective-permute-done | bytes 73760 | tf_op jit(solution)/shard_map/ppermute | solution.py:221
  11.1 0.6 %shard_map.95 = (bf16[12,24,128]{2,1,0:T(8,128)(2,1)S(1)}, bf16[12,24,128]{2,1,0:T(8,128)(2,1)S(1)}, bf16[12,24,128]{2,1,0:T(8,128)(2,1)S(1)}, bf16[12,24,128]{2,1,0:T(8,128)(2,1)S(1)}) custom-call(bf16[12,24,128]{2,1,0:T(8,128)(2,1)S(1)} %collective-permute-done.refs_0_, f32[1,128]{1,0:T(1,128)S(1)} %get-tuple-element.25.gain_ref.refs_1_, ...), custom_call_target="tpu_custom_call" | custom-call | flops 12800000 | tf_op jit(solution)/shard_map/pallas_call | solution.py:38
  11.8 1.6 %collective-permute-start.4 = (bf16[12,24,128]{2,1,0:T(8,128)(2,1)S(1)}, bf16[12,24,128]{2,1,0:T(8,128)(2,1)S(1)}, u32[]{:S(2)}, u32[]{:S(2)}) collective-permute-start(bf16[12,24,128]{2,1,0:T(8,128)(2,1)S(1)} %get-tuple-element.34), channel_id=1, source_target_pairs={{0,1},{1,0},{2,3},{3,2},{4,5},{5,4},{6,7},{7,6},{8,9},{9,8},{10,11... | collective-permute-start | bytes 221192 | tf_op jit(solution)/shard_map/ppermute | solution.py:221
  13.4 1.2 %collective-permute-start.5 = (bf16[12,24,128]{2,1,0:T(8,128)(2,1)S(1)}, bf16[12,24,128]{2,1,0:T(8,128)(2,1)S(1)}, u32[]{:S(2)}, u32[]{:S(2)}) collective-permute-start(bf16[12,24,128]{2,1,0:T(8,128)(2,1)S(1)} %get-tuple-element.35), channel_id=1, source_target_pairs={{0,9},{1,8},{2,11},{3,10},{4,13},{5,12},{6,15},{7,14},{8,1},{9,0},... | collective-permute-start | bytes 221192 | tf_op jit(solution)/shard_map/ppermute | solution.py:221
  14.6 1.6 %collective-permute-start.6 = (bf16[12,24,128]{2,1,0:T(8,128)(2,1)S(1)}, bf16[12,24,128]{2,1,0:T(8,128)(2,1)S(1)}, u32[]{:S(2)}, u32[]{:S(2)}) collective-permute-start(bf16[12,24,128]{2,1,0:T(8,128)(2,1)S(1)} %get-tuple-element.36), channel_id=1, source_target_pairs={{0,17},{1,16},{2,19},{3,18},{4,21},{5,20},{6,23},{7,22},{8,25},{9,... | collective-permute-start | bytes 221192 | tf_op jit(solution)/shard_map/ppermute | solution.py:221
  16.2 0.2 collective-permute-start.7
  16.3 0.0 collective-permute-done.4.refs_1_
  16.3 1.4 %collective-permute-done.5.refs_2_ = bf16[12,24,128]{2,1,0:T(8,128)(2,1)S(1)} collective-permute-done((bf16[12,24,128]{2,1,0:T(8,128)(2,1)S(1)}, bf16[12,24,128]{2,1,0:T(8,128)(2,1)S(1)}, u32[]{:S(2)}, u32[]{:S(2)}) %collective-permute-start.5) | collective-permute-done | bytes 73760 | tf_op jit(solution)/shard_map/ppermute | solution.py:221
  17.7 0.8 %collective-permute-done.6.refs_3_ = bf16[12,24,128]{2,1,0:T(8,128)(2,1)S(1)} collective-permute-done((bf16[12,24,128]{2,1,0:T(8,128)(2,1)S(1)}, bf16[12,24,128]{2,1,0:T(8,128)(2,1)S(1)}, u32[]{:S(2)}, u32[]{:S(2)}) %collective-permute-start.6) | collective-permute-done | bytes 73760 | tf_op jit(solution)/shard_map/ppermute | solution.py:221
  18.5 2.8 %collective-permute-done.7.refs_4_ = bf16[12,24,128]{2,1,0:T(8,128)(2,1)S(1)} collective-permute-done((bf16[12,24,128]{2,1,0:T(8,128)(2,1)S(1)}, bf16[12,24,128]{2,1,0:T(8,128)(2,1)S(1)}, u32[]{:S(2)}, u32[]{:S(2)}) %collective-permute-start.7) | collective-permute-done | bytes 73760 | tf_op jit(solution)/shard_map/ppermute | solution.py:221
  21.4 0.2 shard_map.96
  21.6 0.2 collective-permute-start.8
  21.8 0.3 %shard_map.97.kept_ref = f32[288,128]{1,0:T(8,128)S(1)} custom-call(bf16[12,16,128]{2,1,0:T(8,128)(2,1)S(1)} %get-tuple-element.41.keep_ref, bf16[2,288,192]{2,1,0:T(8,128)(2,1)S(1)} %get-tuple-element.39.turn_ref, bf16[128,128]{1,0:T(8,128)(2,1)S(1)} %get-tuple-element.40.weight_ref), custom_call_target="tpu_custom_call" | custom-call | flops 4800000 | tf_op jit(solution)/shard_map/pallas_call | solution.py:38
  22.1 0.8 %collective-permute-done.8.come_ref = bf16[12,16,128]{2,1,0:T(8,128)(2,1)S(1)} collective-permute-done((bf16[12,16,128]{2,1,0:T(8,128)(2,1)S(1)}, bf16[12,16,128]{2,1,0:T(8,128)(2,1)S(1)}, u32[]{:S(2)}, u32[]{:S(2)}) %collective-permute-start.8) | collective-permute-done | bytes 49184 | tf_op jit(solution)/shard_map/ppermute | solution.py:221
  22.9 1.0 %shard_map.98 = bf16[12,24,128]{2,1,0:T(8,128)(2,1)} custom-call(bf16[12,16,128]{2,1,0:T(8,128)(2,1)S(1)} %collective-permute-done.8.come_ref, bf16[2,288,192]{2,1,0:T(8,128)(2,1)S(1)} %get-tuple-element.39.turn_ref, bf16[128,128]{1,0:T(8,128)(2,1)S(1)} %get-tuple-element.40.weight_ref, f32[288,128]{1,0:T(8,128)S(1)} %shard_map.97.kept_ref, ...), custom_call_target="tpu_custom_call" | custom-call | flops 8000000 | tf_op jit(solution)/shard_map/pallas_call | solution.py:38
Async XLA Ops:
  0.0 7.2 %collective-permute-start.1 = (bf16[12,24,128]{2,1,0:T(8,128)(2,1)}, bf16[12,24,128]{2,1,0:T(8,128)(2,1)S(1)}, u32[]{:S(2)}, u32[]{:S(2)}) collective-permute-start(bf16[12,24,128]{2,1,0:T(8,128)(2,1)} %bitcast.4), channel_id=1, source_target_pairs={{0,1},{1,0},{2,3},{3,2},{4,5},{5,4},{6,7},{7,6},{8,9},{9,8},{10,11... | collective-permute-start | bytes 221192 | tf_op jit(solution)/shard_map/ppermute | solution.py:221
  0.5 7.4 %collective-permute-start.3 = (bf16[12,24,128]{2,1,0:T(8,128)(2,1)}, bf16[12,24,128]{2,1,0:T(8,128)(2,1)S(1)}, u32[]{:S(2)}, u32[]{:S(2)}) collective-permute-start(bf16[12,24,128]{2,1,0:T(8,128)(2,1)} %bitcast.5), channel_id=1, source_target_pairs={{3,0},{2,1},{1,2},{0,3},{7,4},{6,5},{5,6},{4,7},{11,8},{10,9},{9,1... | collective-permute-start | bytes 221192 | tf_op jit(solution)/shard_map/ppermute | solution.py:221
  3.2 7.0 %collective-permute-start.2 = (bf16[12,24,128]{2,1,0:T(8,128)(2,1)}, bf16[12,24,128]{2,1,0:T(8,128)(2,1)S(1)}, u32[]{:S(2)}, u32[]{:S(2)}) collective-permute-start(bf16[12,24,128]{2,1,0:T(8,128)(2,1)} %bitcast.6), channel_id=1, source_target_pairs={{5,0},{4,1},{7,2},{6,3},{3,4},{2,5},{1,6},{0,7},{13,8},{12,9},{15,... | collective-permute-start | bytes 221192 | tf_op jit(solution)/shard_map/ppermute | solution.py:221
  5.3 5.9 %collective-permute-start = (bf16[12,24,128]{2,1,0:T(8,128)(2,1)}, bf16[12,24,128]{2,1,0:T(8,128)(2,1)S(1)}, u32[]{:S(2)}, u32[]{:S(2)}) collective-permute-start(bf16[12,24,128]{2,1,0:T(8,128)(2,1)} %bitcast.7), channel_id=1, source_target_pairs={{7,0},{6,1},{5,2},{4,3},{1,4},{0,5},{3,6},{2,7},{15,8},{14,9},{13,... | collective-permute-start | bytes 221192 | tf_op jit(solution)/shard_map/ppermute | solution.py:221
  11.8 4.5 %collective-permute-start.4 = (bf16[12,24,128]{2,1,0:T(8,128)(2,1)S(1)}, bf16[12,24,128]{2,1,0:T(8,128)(2,1)S(1)}, u32[]{:S(2)}, u32[]{:S(2)}) collective-permute-start(bf16[12,24,128]{2,1,0:T(8,128)(2,1)S(1)} %get-tuple-element.34), channel_id=1, source_target_pairs={{0,1},{1,0},{2,3},{3,2},{4,5},{5,4},{6,7},{7,6},{8,9},{9,8},{10,11... | collective-permute-start | bytes 221192 | tf_op jit(solution)/shard_map/ppermute | solution.py:221
  13.4 4.3 %collective-permute-start.5 = (bf16[12,24,128]{2,1,0:T(8,128)(2,1)S(1)}, bf16[12,24,128]{2,1,0:T(8,128)(2,1)S(1)}, u32[]{:S(2)}, u32[]{:S(2)}) collective-permute-start(bf16[12,24,128]{2,1,0:T(8,128)(2,1)S(1)} %get-tuple-element.35), channel_id=1, source_target_pairs={{0,9},{1,8},{2,11},{3,10},{4,13},{5,12},{6,15},{7,14},{8,1},{9,0},... | collective-permute-start | bytes 221192 | tf_op jit(solution)/shard_map/ppermute | solution.py:221
  14.6 4.0 %collective-permute-start.6 = (bf16[12,24,128]{2,1,0:T(8,128)(2,1)S(1)}, bf16[12,24,128]{2,1,0:T(8,128)(2,1)S(1)}, u32[]{:S(2)}, u32[]{:S(2)}) collective-permute-start(bf16[12,24,128]{2,1,0:T(8,128)(2,1)S(1)} %get-tuple-element.36), channel_id=1, source_target_pairs={{0,17},{1,16},{2,19},{3,18},{4,21},{5,20},{6,23},{7,22},{8,25},{9,... | collective-permute-start | bytes 221192 | tf_op jit(solution)/shard_map/ppermute | solution.py:221
  16.2 5.2 %collective-permute-start.7 = (bf16[12,24,128]{2,1,0:T(8,128)(2,1)S(1)}, bf16[12,24,128]{2,1,0:T(8,128)(2,1)S(1)}, u32[]{:S(2)}, u32[]{:S(2)}) collective-permute-start(bf16[12,24,128]{2,1,0:T(8,128)(2,1)S(1)} %get-tuple-element.37), channel_id=1, source_target_pairs={{0,25},{1,24},{2,27},{3,26},{4,29},{5,28},{6,31},{7,30},{8,17},{9,... | collective-permute-start | bytes 221192 | tf_op jit(solution)/shard_map/ppermute | solution.py:221
  21.6 1.3 %collective-permute-start.8 = (bf16[12,16,128]{2,1,0:T(8,128)(2,1)S(1)}, bf16[12,16,128]{2,1,0:T(8,128)(2,1)S(1)}, u32[]{:S(2)}, u32[]{:S(2)}) collective-permute-start(bf16[12,16,128]{2,1,0:T(8,128)(2,1)S(1)} %get-tuple-element.38), channel_id=1, source_target_pairs={{0,1},{1,0},{2,3},{3,2},{4,5},{5,4},{6,7},{7,6},{8,9},{9,8},{10,11... | collective-permute-start | bytes 147464 | tf_op jit(solution)/shard_map/ppermute | solution.py:221

commit v4 on v3

--- a/solution.py
+++ b/solution.py
@@ -143,6 +143,11 @@
     mix(part_ref, left_ref, right_ref)
 
 
+def owner(row, a, rows):
+    circle = [place ^ (place >> 1) for place in range(rows)]
+    return circle[(circle.index(row) + a) % rows]
+
+
 def step_between(level, target, levels):
     def place(z):
         return lax.div(z, 2) + lax.rem(z, 2) * (levels // 2)
@@ -164,7 +169,8 @@
     width = all_ref.shape[1]
     for a, out_ref in enumerate(outs):
         for r in range(per_row):
-            s = step_between(level, (row ^ a) * per_row + r, levels)
+            to = sum(jnp.where(row == n, owner(n, a, rows), 0) for n in range(rows))
+            s = step_between(level, to * per_row + r, levels)
             out_ref[pl.ds(r * width, width)] = all_ref[s]
 
 
@@ -296,7 +302,9 @@
     arrived = [along("east", cores, sums[0])]
     for a in range(1, rows):
         moves = [
-            (n * blocks + e, (n ^ a) * blocks + (e ^ 1)) for n in range(rows) for e in range(blocks)
+            (n * blocks + e, owner(n, a, rows) * blocks + (e ^ 1))
+            for n in range(rows)
+            for e in range(blocks)
         ]
         arrived.append(along(("north", "east"), moves, sums[a]))
 

time: 24 us -> 23.1 us (0.963)
  waiting for transfers between devices: 7.88 us -> 6 us
  starting transfers between devices: 10.5 us -> 11.5 us
    ppermute x9, waiting for transfers between devices: 7.88 us -> 6 us  [along(): return lax.ppermute(value, axes, moves)]
    ppermute x9, starting transfers between devices: 10.5 us -> 11.5 us  [along(): return lax.ppermute(value, axes, moves)]
  transfers between devices with their start and end apart: 9 -> 9, of which waited for: 6 -> 6; matrix products, arithmetic and copies ran while one was open for 0% -> 0% of each run, Pallas kernels for 15% -> 16%
where the time goes in v4:
time: 23.1 us; the launch traced here: 22.9 us
  starting transfers between devices  11.5 us (50%)
  waiting for transfers between devices  6 us (26%)
  Pallas kernels  5.37 us (23%)
    ppermute x9, starting transfers between devices, along(): return lax.ppermute(value, axes, moves)  11.5 us
    ppermute x9, waiting for transfers between devices, along(): return lax.ppermute(value, axes, moves)  6 us
    pallas_call x8, Pallas kernels, call(): pl.pallas_call(kernel, out_shape=outs, in_specs=specs, out_specs=tree, sc...  5.37 us
  transfers between devices with their start and end apart: 9, of which 6 were waited for; matrix products, arithmetic and copies ran while one was open for 0% of the time, Pallas kernels for 16%

profile of v4, /device:TPU:0, one launch (start us, length us, event | category | flops | bytes accessed | tf_op | source)
XLA Modules:
  0.0 22.9 jit_solution(14525121581021388457)
XLA Ops:
  0.0 0.5 %collective-permute-start.1 = (bf16[12,24,128]{2,1,0:T(8,128)(2,1)}, bf16[12,24,128]{2,1,0:T(8,128)(2,1)S(1)}, u32[]{:S(2)}, u32[]{:S(2)}) collective-permute-start(bf16[12,24,128]{2,1,0:T(8,128)(2,1)} %bitcast.4), channel_id=1, source_target_pairs={{0,1},{1,0},{2,3},{3,2},{4,5},{5,4},{6,7},{7,6},{8,9},{9,8},{10,11... | collective-permute-start | bytes 221192 | tf_op jit(solution)/shard_map/ppermute | solution.py:227
  0.5 2.7 %collective-permute-start.3 = (bf16[12,24,128]{2,1,0:T(8,128)(2,1)}, bf16[12,24,128]{2,1,0:T(8,128)(2,1)S(1)}, u32[]{:S(2)}, u32[]{:S(2)}) collective-permute-start(bf16[12,24,128]{2,1,0:T(8,128)(2,1)} %bitcast.5), channel_id=1, source_target_pairs={{3,0},{2,1},{1,2},{0,3},{7,4},{6,5},{5,6},{4,7},{11,8},{10,9},{9,1... | collective-permute-start | bytes 221192 | tf_op jit(solution)/shard_map/ppermute | solution.py:227
  3.2 2.1 %collective-permute-start.2 = (bf16[12,24,128]{2,1,0:T(8,128)(2,1)}, bf16[12,24,128]{2,1,0:T(8,128)(2,1)S(1)}, u32[]{:S(2)}, u32[]{:S(2)}) collective-permute-start(bf16[12,24,128]{2,1,0:T(8,128)(2,1)} %bitcast.6), channel_id=1, source_target_pairs={{5,0},{4,1},{7,2},{6,3},{3,4},{2,5},{1,6},{0,7},{13,8},{12,9},{15,... | collective-permute-start | bytes 221192 | tf_op jit(solution)/shard_map/ppermute | solution.py:227
  5.3 0.6 %collective-permute-start = (bf16[12,24,128]{2,1,0:T(8,128)(2,1)}, bf16[12,24,128]{2,1,0:T(8,128)(2,1)S(1)}, u32[]{:S(2)}, u32[]{:S(2)}) collective-permute-start(bf16[12,24,128]{2,1,0:T(8,128)(2,1)} %bitcast.7), channel_id=1, source_target_pairs={{7,0},{6,1},{5,2},{4,3},{1,4},{0,5},{3,6},{2,7},{15,8},{14,9},{13,... | collective-permute-start | bytes 221192 | tf_op jit(solution)/shard_map/ppermute | solution.py:227
  5.8 1.4 %shard_map.91 = (bf16[288,128]{1,0:T(8,128)(2,1)S(1)}, f32[288,128]{1,0:T(8,128)S(1)}, f32[288,128]{1,0:T(8,128)S(1)}, bf16[2,288,192]{2,1,0:T(8,128)(2,1)S(1)},...) custom-call(bf16[12,24,128]{2,1,0:T(8,128)(2,1)} %bitcast.8, ...), custom_call_target="tpu_custom_call" | custom-call | flops 24000000 | tf_op jit(solution)/shard_map/pallas_call | solution.py:38
  7.2 0.0 collective-permute-done.1.x_ref
  7.2 0.7 %shard_map.92 = (f32[24,3,8,128]{3,2,1,0:T(8,128)S(1)}, bf16[12,24,128]{2,1,0:T(8,128)(2,1)S(1)}) custom-call(bf16[12,24,128]{2,1,0:T(8,128)(2,1)S(1)} %collective-permute-done.1.x_ref, f32[1,128]{1,0:T(1,128)S(1)} %get-tuple-element.25.gain_ref.refs_1_, bf16[128,128]{1,0:T(8,128)(2,1)S(1)} %get-tuple-element.26.lw_ref.refs_2_, ...), custom_call_target="tpu_custom_call" | custom-call | flops 16000000 | tf_op jit(solution)/shard_map/pallas_call | solution.py:38
  7.9 0.0 collective-permute-done.3.x_ref
  7.9 0.6 %shard_map.94.refs_7_ = bf16[12,24,128]{2,1,0:T(8,128)(2,1)S(1)} custom-call(bf16[12,24,128]{2,1,0:T(8,128)(2,1)S(1)} %collective-permute-done.3.x_ref, f32[1,128]{1,0:T(1,128)S(1)} %get-tuple-element.25.gain_ref.refs_1_, bf16[128,128]{1,0:T(8,128)(2,1)S(1)} %get-tuple-element.26.lw_ref.refs_2_, bf16[128,128]{1,0:T(8,128)(2,1)S(1)} %get-tuple-element.27.lg_ref.refs_3_, ...), custom_call_target="tpu_custom_call" | custom-call | flops 9600000 | tf_op jit(solution)/shard_map/pallas_call | solution.py:38
  8.5 1.7 %collective-permute-done.2.x_ref = bf16[12,24,128]{2,1,0:T(8,128)(2,1)S(1)} collective-permute-done((bf16[12,24,128]{2,1,0:T(8,128)(2,1)}, bf16[12,24,128]{2,1,0:T(8,128)(2,1)S(1)}, u32[]{:S(2)}, u32[]{:S(2)}) %collective-permute-start.2) | collective-permute-done | bytes 73760 | tf_op jit(solution)/shard_map/ppermute | solution.py:227
  10.2 0.6 %shard_map.93.refs_6_ = bf16[12,24,128]{2,1,0:T(8,128)(2,1)S(1)} custom-call(bf16[12,24,128]{2,1,0:T(8,128)(2,1)S(1)} %collective-permute-done.2.x_ref, f32[1,128]{1,0:T(1,128)S(1)} %get-tuple-element.25.gain_ref.refs_1_, bf16[128,128]{1,0:T(8,128)(2,1)S(1)} %get-tuple-element.26.lw_ref.refs_2_, bf16[128,128]{1,0:T(8,128)(2,1)S(1)} %get-tuple-element.27.lg_ref.refs_3_, ...), custom_call_target="tpu_custom_call" | custom-call | flops 9600000 | tf_op jit(solution)/shard_map/pallas_call | solution.py:38
  10.8 0.4 %collective-permute-done.refs_0_ = bf16[12,24,128]{2,1,0:T(8,128)(2,1)S(1)} collective-permute-done((bf16[12,24,128]{2,1,0:T(8,128)(2,1)}, bf16[12,24,128]{2,1,0:T(8,128)(2,1)S(1)}, u32[]{:S(2)}, u32[]{:S(2)}) %collective-permute-start) | collective-permute-done | bytes 73760 | tf_op jit(solution)/shard_map/ppermute | solution.py:227
  11.1 0.6 %shard_map.95 = (bf16[12,24,128]{2,1,0:T(8,128)(2,1)S(1)}, bf16[12,24,128]{2,1,0:T(8,128)(2,1)S(1)}, bf16[12,24,128]{2,1,0:T(8,128)(2,1)S(1)}, bf16[12,24,128]{2,1,0:T(8,128)(2,1)S(1)}) custom-call(bf16[12,24,128]{2,1,0:T(8,128)(2,1)S(1)} %collective-permute-done.refs_0_, f32[1,128]{1,0:T(1,128)S(1)} %get-tuple-element.25.gain_ref.refs_1_, ...), custom_call_target="tpu_custom_call" | custom-call | flops 12800000 | tf_op jit(solution)/shard_map/pallas_call | solution.py:38
  11.8 1.6 %collective-permute-start.4 = (bf16[12,24,128]{2,1,0:T(8,128)(2,1)S(1)}, bf16[12,24,128]{2,1,0:T(8,128)(2,1)S(1)}, u32[]{:S(2)}, u32[]{:S(2)}) collective-permute-start(bf16[12,24,128]{2,1,0:T(8,128)(2,1)S(1)} %get-tuple-element.34), channel_id=1, source_target_pairs={{0,1},{1,0},{2,3},{3,2},{4,5},{5,4},{6,7},{7,6},{8,9},{9,8},{10,11... | collective-permute-start | bytes 221192 | tf_op jit(solution)/shard_map/ppermute | solution.py:227
  13.4 1.2 %collective-permute-start.5 = (bf16[12,24,128]{2,1,0:T(8,128)(2,1)S(1)}, bf16[12,24,128]{2,1,0:T(8,128)(2,1)S(1)}, u32[]{:S(2)}, u32[]{:S(2)}) collective-permute-start(bf16[12,24,128]{2,1,0:T(8,128)(2,1)S(1)} %get-tuple-element.35), channel_id=1, source_target_pairs={{0,9},{1,8},{2,11},{3,10},{4,13},{5,12},{6,15},{7,14},{8,25},{9,24... | collective-permute-start | bytes 221192 | tf_op jit(solution)/shard_map/ppermute | solution.py:227
  14.6 1.5 %collective-permute-start.6 = (bf16[12,24,128]{2,1,0:T(8,128)(2,1)S(1)}, bf16[12,24,128]{2,1,0:T(8,128)(2,1)S(1)}, u32[]{:S(2)}, u32[]{:S(2)}) collective-permute-start(bf16[12,24,128]{2,1,0:T(8,128)(2,1)S(1)} %get-tuple-element.36), channel_id=1, source_target_pairs={{0,25},{1,24},{2,27},{3,26},{4,29},{5,28},{6,31},{7,30},{8,17},{9,... | collective-permute-start | bytes 221192 | tf_op jit(solution)/shard_map/ppermute | solution.py:227
  16.1 1.2 %collective-permute-start.7 = (bf16[12,24,128]{2,1,0:T(8,128)(2,1)S(1)}, bf16[12,24,128]{2,1,0:T(8,128)(2,1)S(1)}, u32[]{:S(2)}, u32[]{:S(2)}) collective-permute-start(bf16[12,24,128]{2,1,0:T(8,128)(2,1)S(1)} %get-tuple-element.37), channel_id=1, source_target_pairs={{0,17},{1,16},{2,19},{3,18},{4,21},{5,20},{6,23},{7,22},{8,1},{9,0... | collective-permute-start | bytes 221192 | tf_op jit(solution)/shard_map/ppermute | solution.py:227
  17.3 0.0 collective-permute-done.4.refs_1_
  17.3 0.4 %collective-permute-done.5.refs_2_ = bf16[12,24,128]{2,1,0:T(8,128)(2,1)S(1)} collective-permute-done((bf16[12,24,128]{2,1,0:T(8,128)(2,1)S(1)}, bf16[12,24,128]{2,1,0:T(8,128)(2,1)S(1)}, u32[]{:S(2)}, u32[]{:S(2)}) %collective-permute-start.5) | collective-permute-done | bytes 73760 | tf_op jit(solution)/shard_map/ppermute | solution.py:227
  17.7 2.5 %collective-permute-done.6.refs_3_ = bf16[12,24,128]{2,1,0:T(8,128)(2,1)S(1)} collective-permute-done((bf16[12,24,128]{2,1,0:T(8,128)(2,1)S(1)}, bf16[12,24,128]{2,1,0:T(8,128)(2,1)S(1)}, u32[]{:S(2)}, u32[]{:S(2)}) %collective-permute-start.6) | collective-permute-done | bytes 73760 | tf_op jit(solution)/shard_map/ppermute | solution.py:227
  20.3 0.2 collective-permute-done.7.refs_4_
  20.5 0.2 shard_map.96
  20.7 0.2 collective-permute-start.8
  20.9 0.3 %shard_map.97.kept_ref = f32[288,128]{1,0:T(8,128)S(1)} custom-call(bf16[12,16,128]{2,1,0:T(8,128)(2,1)S(1)} %get-tuple-element.41.keep_ref, bf16[2,288,192]{2,1,0:T(8,128)(2,1)S(1)} %get-tuple-element.39.turn_ref, bf16[128,128]{1,0:T(8,128)(2,1)S(1)} %get-tuple-element.40.weight_ref), custom_call_target="tpu_custom_call" | custom-call | flops 4800000 | tf_op jit(solution)/shard_map/pallas_call | solution.py:38
  21.2 0.8 %collective-permute-done.8.come_ref = bf16[12,16,128]{2,1,0:T(8,128)(2,1)S(1)} collective-permute-done((bf16[12,16,128]{2,1,0:T(8,128)(2,1)S(1)}, bf16[12,16,128]{2,1,0:T(8,128)(2,1)S(1)}, u32[]{:S(2)}, u32[]{:S(2)}) %collective-permute-start.8) | collective-permute-done | bytes 49184 | tf_op jit(solution)/shard_map/ppermute | solution.py:227
  22.0 1.0 %shard_map.98 = bf16[12,24,128]{2,1,0:T(8,128)(2,1)} custom-call(bf16[12,16,128]{2,1,0:T(8,128)(2,1)S(1)} %collective-permute-done.8.come_ref, bf16[2,288,192]{2,1,0:T(8,128)(2,1)S(1)} %get-tuple-element.39.turn_ref, bf16[128,128]{1,0:T(8,128)(2,1)S(1)} %get-tuple-element.40.weight_ref, f32[288,128]{1,0:T(8,128)S(1)} %shard_map.97.kept_ref, ...), custom_call_target="tpu_custom_call" | custom-call | flops 8000000 | tf_op jit(solution)/shard_map/pallas_call | solution.py:38
Async XLA Ops:
  0.0 7.2 %collective-permute-start.1 = (bf16[12,24,128]{2,1,0:T(8,128)(2,1)}, bf16[12,24,128]{2,1,0:T(8,128)(2,1)S(1)}, u32[]{:S(2)}, u32[]{:S(2)}) collective-permute-start(bf16[12,24,128]{2,1,0:T(8,128)(2,1)} %bitcast.4), channel_id=1, source_target_pairs={{0,1},{1,0},{2,3},{3,2},{4,5},{5,4},{6,7},{7,6},{8,9},{9,8},{10,11... | collective-permute-start | bytes 221192 | tf_op jit(solution)/shard_map/ppermute | solution.py:227
  0.5 7.4 %collective-permute-start.3 = (bf16[12,24,128]{2,1,0:T(8,128)(2,1)}, bf16[12,24,128]{2,1,0:T(8,128)(2,1)S(1)}, u32[]{:S(2)}, u32[]{:S(2)}) collective-permute-start(bf16[12,24,128]{2,1,0:T(8,128)(2,1)} %bitcast.5), channel_id=1, source_target_pairs={{3,0},{2,1},{1,2},{0,3},{7,4},{6,5},{5,6},{4,7},{11,8},{10,9},{9,1... | collective-permute-start | bytes 221192 | tf_op jit(solution)/shard_map/ppermute | solution.py:227
  3.2 7.0 %collective-permute-start.2 = (bf16[12,24,128]{2,1,0:T(8,128)(2,1)}, bf16[12,24,128]{2,1,0:T(8,128)(2,1)S(1)}, u32[]{:S(2)}, u32[]{:S(2)}) collective-permute-start(bf16[12,24,128]{2,1,0:T(8,128)(2,1)} %bitcast.6), channel_id=1, source_target_pairs={{5,0},{4,1},{7,2},{6,3},{3,4},{2,5},{1,6},{0,7},{13,8},{12,9},{15,... | collective-permute-start | bytes 221192 | tf_op jit(solution)/shard_map/ppermute | solution.py:227
  5.3 5.9 %collective-permute-start = (bf16[12,24,128]{2,1,0:T(8,128)(2,1)}, bf16[12,24,128]{2,1,0:T(8,128)(2,1)S(1)}, u32[]{:S(2)}, u32[]{:S(2)}) collective-permute-start(bf16[12,24,128]{2,1,0:T(8,128)(2,1)} %bitcast.7), channel_id=1, source_target_pairs={{7,0},{6,1},{5,2},{4,3},{1,4},{0,5},{3,6},{2,7},{15,8},{14,9},{13,... | collective-permute-start | bytes 221192 | tf_op jit(solution)/shard_map/ppermute | solution.py:227
  11.8 5.5 %collective-permute-start.4 = (bf16[12,24,128]{2,1,0:T(8,128)(2,1)S(1)}, bf16[12,24,128]{2,1,0:T(8,128)(2,1)S(1)}, u32[]{:S(2)}, u32[]{:S(2)}) collective-permute-start(bf16[12,24,128]{2,1,0:T(8,128)(2,1)S(1)} %get-tuple-element.34), channel_id=1, source_target_pairs={{0,1},{1,0},{2,3},{3,2},{4,5},{5,4},{6,7},{7,6},{8,9},{9,8},{10,11... | collective-permute-start | bytes 221192 | tf_op jit(solution)/shard_map/ppermute | solution.py:227
  13.4 4.3 %collective-permute-start.5 = (bf16[12,24,128]{2,1,0:T(8,128)(2,1)S(1)}, bf16[12,24,128]{2,1,0:T(8,128)(2,1)S(1)}, u32[]{:S(2)}, u32[]{:S(2)}) collective-permute-start(bf16[12,24,128]{2,1,0:T(8,128)(2,1)S(1)} %get-tuple-element.35), channel_id=1, source_target_pairs={{0,9},{1,8},{2,11},{3,10},{4,13},{5,12},{6,15},{7,14},{8,25},{9,24... | collective-permute-start | bytes 221192 | tf_op jit(solution)/shard_map/ppermute | solution.py:227
  14.6 5.7 %collective-permute-start.6 = (bf16[12,24,128]{2,1,0:T(8,128)(2,1)S(1)}, bf16[12,24,128]{2,1,0:T(8,128)(2,1)S(1)}, u32[]{:S(2)}, u32[]{:S(2)}) collective-permute-start(bf16[12,24,128]{2,1,0:T(8,128)(2,1)S(1)} %get-tuple-element.36), channel_id=1, source_target_pairs={{0,25},{1,24},{2,27},{3,26},{4,29},{5,28},{6,31},{7,30},{8,17},{9,... | collective-permute-start | bytes 221192 | tf_op jit(solution)/shard_map/ppermute | solution.py:227
  16.1 4.3 %collective-permute-start.7 = (bf16[12,24,128]{2,1,0:T(8,128)(2,1)S(1)}, bf16[12,24,128]{2,1,0:T(8,128)(2,1)S(1)}, u32[]{:S(2)}, u32[]{:S(2)}) collective-permute-start(bf16[12,24,128]{2,1,0:T(8,128)(2,1)S(1)} %get-tuple-element.37), channel_id=1, source_target_pairs={{0,17},{1,16},{2,19},{3,18},{4,21},{5,20},{6,23},{7,22},{8,1},{9,0... | collective-permute-start | bytes 221192 | tf_op jit(solution)/shard_map/ppermute | solution.py:227
  20.7 1.3 %collective-permute-start.8 = (bf16[12,16,128]{2,1,0:T(8,128)(2,1)S(1)}, bf16[12,16,128]{2,1,0:T(8,128)(2,1)S(1)}, u32[]{:S(2)}, u32[]{:S(2)}) collective-permute-start(bf16[12,16,128]{2,1,0:T(8,128)(2,1)S(1)} %get-tuple-element.38), channel_id=1, source_target_pairs={{0,1},{1,0},{2,3},{3,2},{4,5},{5,4},{6,7},{7,6},{8,9},{9,8},{10,11... | collective-permute-start | bytes 147464 | tf_op jit(solution)/shard_map/ppermute | solution.py:227

commit v5 on v3

--- a/solution.py
+++ b/solution.py
@@ -168,17 +168,18 @@
             out_ref[pl.ds(r * width, width)] = all_ref[s]
 
 
-def sum_kernel(scale, gain_ref, *refs):
+def sum_kernel(scale, gain_ref, weight_ref, *refs):
     parts, (keep_ref, send_ref) = refs[:-2], refs[-2:]
     total = parts[0][...].astype(F32)
     for ref in parts[1:]:
         total = total + ref[...].astype(F32)
     mixed = (total * scale).astype(BF16).astype(F32)
-    channels = mixed.shape[2]
+    rows, _, channels = mixed.shape
     scaled = scale_channels(mixed, gain_ref[...].reshape(1, 1, channels)).astype(BF16)
     pitch = keep_ref.shape[1]
     keep_ref[...] = scaled[:, :pitch]
-    send_ref[...] = scaled[:, scaled.shape[1] - pitch :]
+    half = scaled[:, scaled.shape[1] - pitch :].reshape(rows * pitch, channels)
+    send_ref[...] = dot(half, weight_ref[...]).astype(BF16).reshape(send_ref.shape)
 
 
 def turned(half_ref, turn_ref, which, weight_ref):
@@ -191,8 +192,10 @@
     out_ref[...] = turned(keep_ref, turn_ref, 0, weight_ref)
 
 
-def out_kernel(come_ref, turn_ref, weight_ref, kept_ref, gate_ref, out_ref):
-    out = (kept_ref[...] + turned(come_ref, turn_ref, 1, weight_ref)) * gate_ref[...]
+def out_kernel(come_ref, turn_ref, kept_ref, gate_ref, out_ref):
+    rows, pitch, channels = come_ref.shape
+    come = come_ref[...].reshape(rows * pitch, channels)
+    out = (kept_ref[...] + dot(turn_ref[1], come)) * gate_ref[...]
     out_ref[...] = out.astype(BF16).reshape(out_ref.shape)
 
 
@@ -304,15 +307,15 @@
     scale = (height * rows) ** (-0.5)
     keep, send = call(
         lambda *refs: sum_kernel(scale, *refs),
-        (half, half),
-        [VMEM] * (1 + rows),
-        (mid, *arrived),
+        (half, shape((part_rows, pitch, channels))),
+        [VMEM] * (2 + rows),
+        (mid, ow, *arrived),
         0.3,
     )
     come = along("east", cores, send)
     kept = call(keep_kernel, shape((pairs, channels), F32), [VMEM] * 3, (keep, turn, ow), 0.3)
     out = call(
-        out_kernel, shape((width, height, channels)), [VMEM] * 5, (come, turn, ow, kept, gate), 0.5
+        out_kernel, shape((width, height, channels)), [VMEM] * 4, (come, turn, kept, gate), 0.5
     )
     return jnp.transpose(out, (1, 0, 2))
 

time: 24 us -> 24 us (level)
  no operation moved by 1% of the time
where the time goes in v5:
time: 24 us; the launch traced here: 23.8 us
  starting transfers between devices  10.5 us (44%)
  waiting for transfers between devices  7.88 us (33%)
  Pallas kernels  5.33 us (22%)
    ppermute x9, starting transfers between devices, along(): return lax.ppermute(value, axes, moves)  10.5 us
    ppermute x9, waiting for transfers between devices, along(): return lax.ppermute(value, axes, moves)  7.88 us
    pallas_call x8, Pallas kernels, call(): pl.pallas_call(kernel, out_shape=outs, in_specs=specs, out_specs=tree, sc...  5.33 us
  transfers between devices with their start and end apart: 9, of which 6 were waited for; matrix products, arithmetic and copies ran while one was open for 0% of the time, Pallas kernels for 15%

profile of v5, /device:TPU:0, one launch (start us, length us, event | category | flops | bytes accessed | tf_op | source)
XLA Modules:
  0.0 23.8 jit_solution(11617626459478928752)
XLA Ops:
  0.0 0.5 %collective-permute-start.1 = (bf16[12,24,128]{2,1,0:T(8,128)(2,1)}, bf16[12,24,128]{2,1,0:T(8,128)(2,1)S(1)}, u32[]{:S(2)}, u32[]{:S(2)}) collective-permute-start(bf16[12,24,128]{2,1,0:T(8,128)(2,1)} %bitcast.4), channel_id=1, source_target_pairs={{0,1},{1,0},{2,3},{3,2},{4,5},{5,4},{6,7},{7,6},{8,9},{9,8},{10,11... | collective-permute-start | bytes 221192 | tf_op jit(solution)/shard_map/ppermute | solution.py:224
  0.5 2.7 %collective-permute-start.3 = (bf16[12,24,128]{2,1,0:T(8,128)(2,1)}, bf16[12,24,128]{2,1,0:T(8,128)(2,1)S(1)}, u32[]{:S(2)}, u32[]{:S(2)}) collective-permute-start(bf16[12,24,128]{2,1,0:T(8,128)(2,1)} %bitcast.5), channel_id=1, source_target_pairs={{3,0},{2,1},{1,2},{0,3},{7,4},{6,5},{5,6},{4,7},{11,8},{10,9},{9,1... | collective-permute-start | bytes 221192 | tf_op jit(solution)/shard_map/ppermute | solution.py:224
  3.2 2.1 %collective-permute-start.2 = (bf16[12,24,128]{2,1,0:T(8,128)(2,1)}, bf16[12,24,128]{2,1,0:T(8,128)(2,1)S(1)}, u32[]{:S(2)}, u32[]{:S(2)}) collective-permute-start(bf16[12,24,128]{2,1,0:T(8,128)(2,1)} %bitcast.6), channel_id=1, source_target_pairs={{5,0},{4,1},{7,2},{6,3},{3,4},{2,5},{1,6},{0,7},{13,8},{12,9},{15,... | collective-permute-start | bytes 221192 | tf_op jit(solution)/shard_map/ppermute | solution.py:224
  5.3 0.6 %collective-permute-start = (bf16[12,24,128]{2,1,0:T(8,128)(2,1)}, bf16[12,24,128]{2,1,0:T(8,128)(2,1)S(1)}, u32[]{:S(2)}, u32[]{:S(2)}) collective-permute-start(bf16[12,24,128]{2,1,0:T(8,128)(2,1)} %bitcast.7), channel_id=1, source_target_pairs={{7,0},{6,1},{5,2},{4,3},{1,4},{0,5},{3,6},{2,7},{15,8},{14,9},{13,... | collective-permute-start | bytes 221192 | tf_op jit(solution)/shard_map/ppermute | solution.py:224
  5.8 1.4 %shard_map.91 = (bf16[288,128]{1,0:T(8,128)(2,1)S(1)}, f32[288,128]{1,0:T(8,128)S(1)}, f32[288,128]{1,0:T(8,128)S(1)}, bf16[2,288,192]{2,1,0:T(8,128)(2,1)S(1)},...) custom-call(bf16[12,24,128]{2,1,0:T(8,128)(2,1)} %bitcast.8, ...), custom_call_target="tpu_custom_call" | custom-call | flops 24000000 | tf_op jit(solution)/shard_map/pallas_call | solution.py:38
  7.2 0.0 collective-permute-done.1.x_ref
  7.2 0.7 %shard_map.92 = (f32[24,3,8,128]{3,2,1,0:T(8,128)S(1)}, bf16[12,24,128]{2,1,0:T(8,128)(2,1)S(1)}) custom-call(bf16[12,24,128]{2,1,0:T(8,128)(2,1)S(1)} %collective-permute-done.1.x_ref, f32[1,128]{1,0:T(1,128)S(1)} %get-tuple-element.26.gain_ref.refs_1_, bf16[128,128]{1,0:T(8,128)(2,1)S(1)} %get-tuple-element.27.lw_ref.refs_2_, ...), custom_call_target="tpu_custom_call" | custom-call | flops 16000000 | tf_op jit(solution)/shard_map/pallas_call | solution.py:38
  7.9 0.0 collective-permute-done.3.x_ref
  7.9 0.6 %shard_map.94.refs_7_ = bf16[12,24,128]{2,1,0:T(8,128)(2,1)S(1)} custom-call(bf16[12,24,128]{2,1,0:T(8,128)(2,1)S(1)} %collective-permute-done.3.x_ref, f32[1,128]{1,0:T(1,128)S(1)} %get-tuple-element.26.gain_ref.refs_1_, bf16[128,128]{1,0:T(8,128)(2,1)S(1)} %get-tuple-element.27.lw_ref.refs_2_, bf16[128,128]{1,0:T(8,128)(2,1)S(1)} %get-tuple-element.28.lg_ref.refs_3_, ...), custom_call_target="tpu_custom_call" | custom-call | flops 9600000 | tf_op jit(solution)/shard_map/pallas_call | solution.py:38
  8.5 1.7 %collective-permute-done.2.x_ref = bf16[12,24,128]{2,1,0:T(8,128)(2,1)S(1)} collective-permute-done((bf16[12,24,128]{2,1,0:T(8,128)(2,1)}, bf16[12,24,128]{2,1,0:T(8,128)(2,1)S(1)}, u32[]{:S(2)}, u32[]{:S(2)}) %collective-permute-start.2) | collective-permute-done | bytes 73760 | tf_op jit(solution)/shard_map/ppermute | solution.py:224
  10.2 0.6 %shard_map.93.refs_6_ = bf16[12,24,128]{2,1,0:T(8,128)(2,1)S(1)} custom-call(bf16[12,24,128]{2,1,0:T(8,128)(2,1)S(1)} %collective-permute-done.2.x_ref, f32[1,128]{1,0:T(1,128)S(1)} %get-tuple-element.26.gain_ref.refs_1_, bf16[128,128]{1,0:T(8,128)(2,1)S(1)} %get-tuple-element.27.lw_ref.refs_2_, bf16[128,128]{1,0:T(8,128)(2,1)S(1)} %get-tuple-element.28.lg_ref.refs_3_, ...), custom_call_target="tpu_custom_call" | custom-call | flops 9600000 | tf_op jit(solution)/shard_map/pallas_call | solution.py:38
  10.8 0.4 %collective-permute-done.refs_0_ = bf16[12,24,128]{2,1,0:T(8,128)(2,1)S(1)} collective-permute-done((bf16[12,24,128]{2,1,0:T(8,128)(2,1)}, bf16[12,24,128]{2,1,0:T(8,128)(2,1)S(1)}, u32[]{:S(2)}, u32[]{:S(2)}) %collective-permute-start) | collective-permute-done | bytes 73760 | tf_op jit(solution)/shard_map/ppermute | solution.py:224
  11.1 0.6 %shard_map.95 = (bf16[12,24,128]{2,1,0:T(8,128)(2,1)S(1)}, bf16[12,24,128]{2,1,0:T(8,128)(2,1)S(1)}, bf16[12,24,128]{2,1,0:T(8,128)(2,1)S(1)}, bf16[12,24,128]{2,1,0:T(8,128)(2,1)S(1)}) custom-call(bf16[12,24,128]{2,1,0:T(8,128)(2,1)S(1)} %collective-permute-done.refs_0_, f32[1,128]{1,0:T(1,128)S(1)} %get-tuple-element.26.gain_ref.refs_1_, ...), custom_call_target="tpu_custom_call" | custom-call | flops 12800000 | tf_op jit(solution)/shard_map/pallas_call | solution.py:38
  11.8 1.6 %collective-permute-start.4 = (bf16[12,24,128]{2,1,0:T(8,128)(2,1)S(1)}, bf16[12,24,128]{2,1,0:T(8,128)(2,1)S(1)}, u32[]{:S(2)}, u32[]{:S(2)}) collective-permute-start(bf16[12,24,128]{2,1,0:T(8,128)(2,1)S(1)} %get-tuple-element.35), channel_id=1, source_target_pairs={{0,1},{1,0},{2,3},{3,2},{4,5},{5,4},{6,7},{7,6},{8,9},{9,8},{10,11... | collective-permute-start | bytes 221192 | tf_op jit(solution)/shard_map/ppermute | solution.py:224
  13.4 1.2 %collective-permute-start.5 = (bf16[12,24,128]{2,1,0:T(8,128)(2,1)S(1)}, bf16[12,24,128]{2,1,0:T(8,128)(2,1)S(1)}, u32[]{:S(2)}, u32[]{:S(2)}) collective-permute-start(bf16[12,24,128]{2,1,0:T(8,128)(2,1)S(1)} %get-tuple-element.36), channel_id=1, source_target_pairs={{0,9},{1,8},{2,11},{3,10},{4,13},{5,12},{6,15},{7,14},{8,1},{9,0},... | collective-permute-start | bytes 221192 | tf_op jit(solution)/shard_map/ppermute | solution.py:224
  14.6 1.6 %collective-permute-start.6 = (bf16[12,24,128]{2,1,0:T(8,128)(2,1)S(1)}, bf16[12,24,128]{2,1,0:T(8,128)(2,1)S(1)}, u32[]{:S(2)}, u32[]{:S(2)}) collective-permute-start(bf16[12,24,128]{2,1,0:T(8,128)(2,1)S(1)} %get-tuple-element.37), channel_id=1, source_target_pairs={{0,17},{1,16},{2,19},{3,18},{4,21},{5,20},{6,23},{7,22},{8,25},{9,... | collective-permute-start | bytes 221192 | tf_op jit(solution)/shard_map/ppermute | solution.py:224
  16.2 0.2 collective-permute-start.7
  16.3 0.0 collective-permute-done.4.refs_2_
  16.3 1.4 %collective-permute-done.5.refs_3_ = bf16[12,24,128]{2,1,0:T(8,128)(2,1)S(1)} collective-permute-done((bf16[12,24,128]{2,1,0:T(8,128)(2,1)S(1)}, bf16[12,24,128]{2,1,0:T(8,128)(2,1)S(1)}, u32[]{:S(2)}, u32[]{:S(2)}) %collective-permute-start.5) | collective-permute-done | bytes 73760 | tf_op jit(solution)/shard_map/ppermute | solution.py:224
  17.7 0.8 %collective-permute-done.6.refs_4_ = bf16[12,24,128]{2,1,0:T(8,128)(2,1)S(1)} collective-permute-done((bf16[12,24,128]{2,1,0:T(8,128)(2,1)S(1)}, bf16[12,24,128]{2,1,0:T(8,128)(2,1)S(1)}, u32[]{:S(2)}, u32[]{:S(2)}) %collective-permute-start.6) | collective-permute-done | bytes 73760 | tf_op jit(solution)/shard_map/ppermute | solution.py:224
  18.5 2.8 %collective-permute-done.7.refs_5_ = bf16[12,24,128]{2,1,0:T(8,128)(2,1)S(1)} collective-permute-done((bf16[12,24,128]{2,1,0:T(8,128)(2,1)S(1)}, bf16[12,24,128]{2,1,0:T(8,128)(2,1)S(1)}, u32[]{:S(2)}, u32[]{:S(2)}) %collective-permute-start.7) | collective-permute-done | bytes 73760 | tf_op jit(solution)/shard_map/ppermute | solution.py:224
  21.4 0.3 %shard_map.96 = (bf16[12,16,128]{2,1,0:T(8,128)(2,1)S(1)}, bf16[12,16,128]{2,1,0:T(8,128)(2,1)S(1)}) custom-call(f32[1,128]{1,0:T(1,128)S(1)} %get-tuple-element.24.refs_0_, bf16[128,128]{1,0:T(8,128)(2,1)S(1)} %get-tuple-element.25.refs_1_.weight_ref, bf16[12,24,128]{2,1,0:T(8,128)(2,1)S(1)} %collective-permute-done.4.refs_2_, ...), custom_call_target="tpu_custom_call" | custom-call | flops 4800000 | tf_op jit(solution)/shard_map/pallas_call | solution.py:38
  21.7 0.2 collective-permute-start.8
  21.9 0.3 %shard_map.97.kept_ref = f32[288,128]{1,0:T(8,128)S(1)} custom-call(bf16[12,16,128]{2,1,0:T(8,128)(2,1)S(1)} %get-tuple-element.41.keep_ref, bf16[2,288,192]{2,1,0:T(8,128)(2,1)S(1)} %get-tuple-element.40.turn_ref, bf16[128,128]{1,0:T(8,128)(2,1)S(1)} %get-tuple-element.25.refs_1_.weight_ref), custom_call_target="tpu_custom_call" | custom-call | flops 4800000 | tf_op jit(solution)/shard_map/pallas_call | solution.py:38
  22.2 0.8 %collective-permute-done.8.come_ref = bf16[12,16,128]{2,1,0:T(8,128)(2,1)S(1)} collective-permute-done((bf16[12,16,128]{2,1,0:T(8,128)(2,1)S(1)}, bf16[12,16,128]{2,1,0:T(8,128)(2,1)S(1)}, u32[]{:S(2)}, u32[]{:S(2)}) %collective-permute-start.8) | collective-permute-done | bytes 49184 | tf_op jit(solution)/shard_map/ppermute | solution.py:224
  23.0 0.8 %shard_map.98 = bf16[12,24,128]{2,1,0:T(8,128)(2,1)} custom-call(bf16[12,16,128]{2,1,0:T(8,128)(2,1)S(1)} %collective-permute-done.8.come_ref, bf16[2,288,192]{2,1,0:T(8,128)(2,1)S(1)} %get-tuple-element.40.turn_ref, f32[288,128]{1,0:T(8,128)S(1)} %shard_map.97.kept_ref, f32[288,128]{1,0:T(8,128)S(1)} %get-tuple-element.42.gate_ref), custom_call_target="tpu_custom_call" | custom-call | flops 8000000 | tf_op jit(solution)/shard_map/pallas_call | solution.py:38
Async XLA Ops:
  0.0 7.2 %collective-permute-start.1 = (bf16[12,24,128]{2,1,0:T(8,128)(2,1)}, bf16[12,24,128]{2,1,0:T(8,128)(2,1)S(1)}, u32[]{:S(2)}, u32[]{:S(2)}) collective-permute-start(bf16[12,24,128]{2,1,0:T(8,128)(2,1)} %bitcast.4), channel_id=1, source_target_pairs={{0,1},{1,0},{2,3},{3,2},{4,5},{5,4},{6,7},{7,6},{8,9},{9,8},{10,11... | collective-permute-start | bytes 221192 | tf_op jit(solution)/shard_map/ppermute | solution.py:224
  0.5 7.4 %collective-permute-start.3 = (bf16[12,24,128]{2,1,0:T(8,128)(2,1)}, bf16[12,24,128]{2,1,0:T(8,128)(2,1)S(1)}, u32[]{:S(2)}, u32[]{:S(2)}) collective-permute-start(bf16[12,24,128]{2,1,0:T(8,128)(2,1)} %bitcast.5), channel_id=1, source_target_pairs={{3,0},{2,1},{1,2},{0,3},{7,4},{6,5},{5,6},{4,7},{11,8},{10,9},{9,1... | collective-permute-start | bytes 221192 | tf_op jit(solution)/shard_map/ppermute | solution.py:224
  3.2 7.0 %collective-permute-start.2 = (bf16[12,24,128]{2,1,0:T(8,128)(2,1)}, bf16[12,24,128]{2,1,0:T(8,128)(2,1)S(1)}, u32[]{:S(2)}, u32[]{:S(2)}) collective-permute-start(bf16[12,24,128]{2,1,0:T(8,128)(2,1)} %bitcast.6), channel_id=1, source_target_pairs={{5,0},{4,1},{7,2},{6,3},{3,4},{2,5},{1,6},{0,7},{13,8},{12,9},{15,... | collective-permute-start | bytes 221192 | tf_op jit(solution)/shard_map/ppermute | solution.py:224
  5.3 5.9 %collective-permute-start = (bf16[12,24,128]{2,1,0:T(8,128)(2,1)}, bf16[12,24,128]{2,1,0:T(8,128)(2,1)S(1)}, u32[]{:S(2)}, u32[]{:S(2)}) collective-permute-start(bf16[12,24,128]{2,1,0:T(8,128)(2,1)} %bitcast.7), channel_id=1, source_target_pairs={{7,0},{6,1},{5,2},{4,3},{1,4},{0,5},{3,6},{2,7},{15,8},{14,9},{13,... | collective-permute-start | bytes 221192 | tf_op jit(solution)/shard_map/ppermute | solution.py:224
  11.8 4.5 %collective-permute-start.4 = (bf16[12,24,128]{2,1,0:T(8,128)(2,1)S(1)}, bf16[12,24,128]{2,1,0:T(8,128)(2,1)S(1)}, u32[]{:S(2)}, u32[]{:S(2)}) collective-permute-start(bf16[12,24,128]{2,1,0:T(8,128)(2,1)S(1)} %get-tuple-element.35), channel_id=1, source_target_pairs={{0,1},{1,0},{2,3},{3,2},{4,5},{5,4},{6,7},{7,6},{8,9},{9,8},{10,11... | collective-permute-start | bytes 221192 | tf_op jit(solution)/shard_map/ppermute | solution.py:224
  13.4 4.3 %collective-permute-start.5 = (bf16[12,24,128]{2,1,0:T(8,128)(2,1)S(1)}, bf16[12,24,128]{2,1,0:T(8,128)(2,1)S(1)}, u32[]{:S(2)}, u32[]{:S(2)}) collective-permute-start(bf16[12,24,128]{2,1,0:T(8,128)(2,1)S(1)} %get-tuple-element.36), channel_id=1, source_target_pairs={{0,9},{1,8},{2,11},{3,10},{4,13},{5,12},{6,15},{7,14},{8,1},{9,0},... | collective-permute-start | bytes 221192 | tf_op jit(solution)/shard_map/ppermute | solution.py:224
  14.6 4.0 %collective-permute-start.6 = (bf16[12,24,128]{2,1,0:T(8,128)(2,1)S(1)}, bf16[12,24,128]{2,1,0:T(8,128)(2,1)S(1)}, u32[]{:S(2)}, u32[]{:S(2)}) collective-permute-start(bf16[12,24,128]{2,1,0:T(8,128)(2,1)S(1)} %get-tuple-element.37), channel_id=1, source_target_pairs={{0,17},{1,16},{2,19},{3,18},{4,21},{5,20},{6,23},{7,22},{8,25},{9,... | collective-permute-start | bytes 221192 | tf_op jit(solution)/shard_map/ppermute | solution.py:224
  16.2 5.2 %collective-permute-start.7 = (bf16[12,24,128]{2,1,0:T(8,128)(2,1)S(1)}, bf16[12,24,128]{2,1,0:T(8,128)(2,1)S(1)}, u32[]{:S(2)}, u32[]{:S(2)}) collective-permute-start(bf16[12,24,128]{2,1,0:T(8,128)(2,1)S(1)} %get-tuple-element.38), channel_id=1, source_target_pairs={{0,25},{1,24},{2,27},{3,26},{4,29},{5,28},{6,31},{7,30},{8,17},{9,... | collective-permute-start | bytes 221192 | tf_op jit(solution)/shard_map/ppermute | solution.py:224
  21.7 1.3 %collective-permute-start.8 = (bf16[12,16,128]{2,1,0:T(8,128)(2,1)S(1)}, bf16[12,16,128]{2,1,0:T(8,128)(2,1)S(1)}, u32[]{:S(2)}, u32[]{:S(2)}) collective-permute-start(bf16[12,16,128]{2,1,0:T(8,128)(2,1)S(1)} %get-tuple-element.39), channel_id=1, source_target_pairs={{0,1},{1,0},{2,3},{3,2},{4,5},{5,4},{6,7},{7,6},{8,9},{9,8},{10,11... | collective-permute-start | bytes 147464 | tf_op jit(solution)/shard_map/ppermute | solution.py:224
